TPU v7x, 1024 devices: a whole 4x4x32 slice. The times are simulated.
1024 devices in a mesh: sfc: 64 (over z, core), lev: 16 (over x, y).
Axes of the slice: x: 4, y: 4, z: 32, core: 2. Of those that a mesh axis runs over, the one named last changes fastest.
Arguments:
- tracer_old: float32 [16, 10, 16, 24576], P('lev', None, None, 'sfc'), may hold values from 0.1 to 2
- air_old: float32 [16, 16, 24576], P('lev', None, 'sfc'), may hold values from 0.3 to 20, as said below
- air_new: float32 [16, 16, 24576], P('lev', None, 'sfc'), may hold values from 0.4 to 20, as said below
- dep_coord: float32 [2, 16, 16, 24576], P(None, 'lev', None, 'sfc'), may hold values from -1 to 1
- dep_slot: int32 [16, 16, 24576], P('lev', None, 'sfc'), may hold values from 0 to 639
- fetch_list: int32 [64, 2, 128], P('sfc'), may hold values from 0 to 383, as said below
Outputs:
- tracer_new: float32 [16, 10, 16, 24576], P('lev', None, None, 'sfc')
Inputs may be any that keep to these rules, and one draw needn't show every extreme that they name: `fetch_list`: side 0 holds distinct indices in [128, 384); side 1 holds distinct indices in [0, 256). `air_old`: positive. `air_new`: positive.
All inputs are finite; a program needn't handle non-finite values.
Results may differ from a plain program's by a relative error of at most 0.0003.
Values sent between devices are 32-bit elements; how exact they have to be, the bound alone decides.
No kernel may reach another device: no remote copies, remote signals or barrier semaphores. Data moves between devices by JAX's collectives and lax.ppermute only.
A program may use at most 32 MiB of HBM per device.

v0:
```python
import functools

import jax
import jax.numpy as jnp
from jax import lax
from jax.sharding import Mesh
from jax.sharding import PartitionSpec as P

BAND = 256
SFC_LEV = ("sfc_0", "sfc_1", "lev_0", "lev_1")
SFC = ("sfc_0", "sfc_1")
LEV = ("lev_0", "lev_1")


NODES = (-1.0, -0.4472135954999579, 0.4472135954999579, 1.0)


def by_axis(shard, axes):
    return functools.reduce(lax.psum, axes, shard)


def padded(block, sides, width):
    for axis, dim in sides:
        count = lax.axis_size(axis)
        forward = [(i, i + 1) for i in range(count - 1)]
        forward.append((count - 1, 0))
        backward = [(target, source) for source, target in forward]
        low = lax.ppermute(
            lax.slice_in_dim(block, block.shape[dim] - width, None, axis=dim), axis, forward
        )
        high = lax.ppermute(lax.slice_in_dim(block, 0, width, axis=dim), axis, backward)
        block = jnp.concatenate([low, block, high], axis=dim)
    return block


def basis(coord):
    terms = []
    for first in range(4):
        term = jnp.ones_like(coord)
        for other in range(4):
            if other != first:
                term = term * (coord - NODES[other]) / (NODES[first] - NODES[other])
        terms.append(term)
    return terms


def pick_rows(table, slots):
    return table[slots]


def on_device(tracer_old, air_old, air_new, dep_coord, dep_slot, fetch_list):
    e_dev = tracer_old.shape[3]
    levels = tracer_old.shape[0]
    tracers = tracer_old.shape[1]
    points = tracer_old.shape[2]
    old_term = jnp.sum(air_old[:, None] * tracer_old, axis=(0, 2, 3))
    old_mass = by_axis(old_term, SFC_LEV)
    extended = padded(tracer_old, ((SFC, 3),), BAND)
    left = jnp.take(extended, fetch_list[0, 0] - (e_dev - BAND), axis=3)
    right = jnp.take(extended, BAND + e_dev + fetch_list[0, 1], axis=3)
    buffer = jnp.concatenate([tracer_old, left, right], axis=3)
    width = buffer.shape[3]
    rows = jnp.transpose(buffer, (0, 3, 1, 2)).reshape(levels, width, tracers * points)
    picked = jax.vmap(pick_rows)(rows, dep_slot)
    picked = picked.reshape(levels, points, e_dev, tracers, 16)
    along_a = basis(dep_coord[0])
    along_b = basis(dep_coord[1])
    stacked = jnp.stack([along_a[j // 4] * along_b[j % 4] for j in range(16)], axis=-1)
    interp = jnp.sum(picked * stacked[:, :, :, None, :], axis=-1)
    low = jnp.min(picked, axis=-1)
    high = jnp.max(picked, axis=-1)
    interp = jnp.transpose(interp, (0, 3, 1, 2))
    low = jnp.transpose(low, (0, 3, 1, 2))
    high = jnp.transpose(high, (0, 3, 1, 2))
    clipped = jnp.clip(interp, low, high)
    mass_new = air_new[:, None]
    clip_term = jnp.sum(mass_new * clipped, axis=(0, 2, 3))
    up_term = jnp.sum(mass_new * (high - clipped), axis=(0, 2, 3))
    down_term = jnp.sum(mass_new * (clipped - low), axis=(0, 2, 3))
    summed = by_axis(jnp.stack([clip_term, up_term, down_term]), SFC_LEV)
    clip_mass = summed[0]
    room_up = summed[1]
    room_down = summed[2]
    shortfall = (old_mass - clip_mass)[None, :, None, None]
    raised = shortfall * (high - clipped) / room_up[None, :, None, None]
    lowered = shortfall * (clipped - low) / room_down[None, :, None, None]
    return clipped + jnp.where(shortfall >= 0, raised, lowered)


def solution(mesh):
    finer = Mesh(mesh.devices.reshape(32, 2, 4, 4), ("sfc_0", "sfc_1", "lev_0", "lev_1"))
    placed = (
        P(LEV, None, None, SFC),
        P(LEV, None, SFC),
        P(LEV, None, SFC),
        P(None, LEV, None, SFC),
        P(LEV, None, SFC),
        P(SFC, None, None),
    )
    return jax.shard_map(
        on_device, mesh=finer, in_specs=placed, out_specs=P(LEV, None, None, SFC), check_vma=False
    )
```

profile of v0, /device:TPU:1, one launch (start us, length us, event | category | flops | bytes accessed | tf_op | source)
XLA Modules:
  0.0 194.3 jit_solution(14407763216557581551)
XLA Ops:
  0.0 1.0 fusion.7
  1.0 3.0 %collective-permute-start = (f32[1,10,16,256]{3,2,1,0:T(8,128)S(1)}, f32[1,10,16,256]{3,2,1,0:T(8,128)S(1)}, u32[]{:S(2)}, u32[]{:S(2)}) collective-permute-start(f32[1,10,16,256]{3,2,1,0:T(8,128)S(1)} %get-tuple-element.27), channel_id=1, source_target_pairs={{0,16},{16,32},{32,48},{48,64},{64,80},{80,96},{96,112},{112,128},... | collective-permute-start | bytes 491528 | tf_op jit(solution)/shard_map/ppermute | solution.py:28
  4.0 11.1 %collective-permute-start.1 = (f32[1,10,16,256]{3,2,1,0:T(8,128)S(1)}, f32[1,10,16,256]{3,2,1,0:T(8,128)S(1)}, u32[]{:S(2)}, u32[]{:S(2)}) collective-permute-start(f32[1,10,16,256]{3,2,1,0:T(8,128)S(1)} %get-tuple-element.28), channel_id=1, source_target_pairs={{16,0},{32,16},{48,32},{64,48},{80,64},{96,80},{112,96},{128,112},... | collective-permute-start | bytes 491528 | tf_op jit(solution)/shard_map/ppermute | solution.py:31
  16.7 0.8 constant_dynamic-update-slice_fusion.15
  17.5 0.8 constant_dynamic-update-slice_fusion.14
  18.3 0.8 constant_dynamic-update-slice_fusion.13
  19.1 0.8 constant_dynamic-update-slice_fusion.12
  19.8 0.8 constant_dynamic-update-slice_fusion.11
  20.6 0.8 constant_dynamic-update-slice_fusion.10
  21.4 0.8 constant_dynamic-update-slice_fusion.9
  22.2 0.8 constant_dynamic-update-slice_fusion.8
  22.9 0.8 constant_dynamic-update-slice_fusion.7
  23.7 0.8 constant_dynamic-update-slice_fusion.6
  25.3 0.8 constant_dynamic-update-slice_fusion.4
  26.1 0.8 constant_dynamic-update-slice_fusion.3
  26.8 0.8 constant_dynamic-update-slice_fusion.2
  27.6 0.8 constant_dynamic-update-slice_fusion.1
  28.4 0.8 constant_dynamic-update-slice_fusion
  29.9 1.1 multiply_reduce_fusion.4
  31.0 1.0 pad_maximum_fusion
  32.0 5.8 %copy.16 = f32[1,10,16,896]{2,1,3,0:T(8,128)} copy(f32[1,10,16,896]{3,2,1,0:T(8,128)S(1)} %pad_maximum_fusion) | data formatting | bytes 1146880 | tf_op jit(solution)/shard_map/concatenate | solution.py:32
  37.9 3.8 %gather_fusion.1 = f32[128,10,16]{2,1,0:T(8,128)S(1)} fusion(f32[10,16,896]{1,0,2:T(8,128)} %bitcast.103, s32[1024]{0:T(1024)S(1)} %pad_clamp_fusion.1), kind=kCustom, calls=%fused_computation.clone | custom fusion | bytes 164352 | tf_op jit(solution)/shard_map/jit(_take)/gather | solution.py:59
  41.7 4.7 %gather_fusion.2 = f32[128,10,16]{2,1,0:T(8,128)} fusion(f32[10,16,896]{1,0,2:T(8,128)} %bitcast.104, s32[1024]{0:T(1024)S(1)} %pad_clamp_fusion), kind=kCustom, calls=%fused_computation.1.clone | custom fusion | bytes 164352 | tf_op jit(solution)/shard_map/jit(_take)/gather | solution.py:60
  46.4 1.6 bitcast_select_fusion
  48.8 57.0 %gather_fusion = f32[6144,160]{1,0:T(8,128)} fusion(f32[1,640,160]{2,1,0:T(8,128)S(1)} %copy.20, s32[6144]{0:T(1024)S(1)} %reshape.935), kind=kCustom, calls=%fused_computation.2 | custom fusion | bytes 7913472 | tf_op jit(solution)/shard_map/vmap()/gather | solution.py:48
  105.8 6.0 %copy.21 = f32[6144,160]{0,1:T(8,128)} copy(f32[6144,160]{1,0:T(8,128)} %gather_fusion) | data formatting | bytes 7864320 | tf_op jit(solution)/shard_map/vmap()/gather | solution.py:48
  111.8 2.9 %copy.22 = f32[20,8,16,384]{3,2,1,0:T(8,128)S(1)} copy(f32[20,8,16,384]{3,1,2,0:T(8,128)} %bitcast.102) | data formatting | bytes 7864320
  115.6 42.8 %all-reduce = (f32[3,10]{1,0:T(4,128)S(1)}, f32[10]{0:T(128)S(1)}) all-reduce(f32[3,10]{1,0:T(4,128)S(1)} %pad_maximum_fusion.2, f32[10]{0:T(128)S(1)} %multiply_reduce_fusion.4), channel_id=1, replica_groups=mesh['sfc_0'=32,'sfc_1'=2,'lev_0'=4,'lev_1'=4] {'sfc_0'}, use_global_device_ids=true, to_apply=%region_11.13 | all-reduce | flops 40 | bytes 320 | tf_op jit(solution)/shard_map/psum | solution.py:19
  158.4 17.9 %all-reduce.3 = (f32[3,10]{1,0:T(4,128)S(1)}, f32[10]{0:T(128)S(1)}) all-reduce(f32[3,10]{1,0:T(4,128)S(1)} %get-tuple-element.12, f32[10]{0:T(128)S(1)} %get-tuple-element.13), channel_id=1, replica_groups=mesh['sfc_0'=32,'sfc_1'=2,'lev_0'=4,'lev_1'=4] {'sfc_1'}, use_global_device_ids=true, to_apply=%region_12.14 | all-reduce | flops 40 | bytes 320 | tf_op jit(solution)/shard_map/psum | solution.py:19
  176.3 8.4 %all-reduce.2 = (f32[3,10]{1,0:T(4,128)S(1)}, f32[10]{0:T(128)S(1)}) all-reduce(f32[3,10]{1,0:T(4,128)S(1)} %get-tuple-element.18, f32[10]{0:T(128)S(1)} %get-tuple-element.19), channel_id=1, replica_groups=mesh['sfc_0'=32,'sfc_1'=2,'lev_0'=4,'lev_1'=4] {'lev_0'}, use_global_device_ids=true, to_apply=%region_13.15 | all-reduce | flops 40 | bytes 320 | tf_op jit(solution)/shard_map/psum | solution.py:19
  184.8 8.7 %all-reduce.1 = (f32[3,10]{1,0:T(4,128)S(1)}, f32[10]{0:T(128)S(1)}) all-reduce(f32[3,10]{1,0:T(4,128)S(1)} %get-tuple-element.16, f32[10]{0:T(128)S(1)} %get-tuple-element.17), channel_id=1, replica_groups=mesh['sfc_0'=32,'sfc_1'=2,'lev_0'=4,'lev_1'=4] {'lev_1'}, use_global_device_ids=true, to_apply=%region_14.16 | all-reduce | flops 40 | bytes 320 | tf_op jit(solution)/shard_map/psum | solution.py:19
  193.5 0.9 select_add_fusion
  (27 shorter events, 4.9 us)
Async XLA Ops:
  1.0 30.0 %collective-permute-start = (f32[1,10,16,256]{3,2,1,0:T(8,128)S(1)}, f32[1,10,16,256]{3,2,1,0:T(8,128)S(1)}, u32[]{:S(2)}, u32[]{:S(2)}) collective-permute-start(f32[1,10,16,256]{3,2,1,0:T(8,128)S(1)} %get-tuple-element.27), channel_id=1, source_target_pairs={{0,16},{16,32},{32,48},{48,64},{64,80},{80,96},{96,112},{112,128},... | collective-permute-start | bytes 491528 | tf_op jit(solution)/shard_map/ppermute | solution.py:28
  4.0 27.0 %collective-permute-start.1 = (f32[1,10,16,256]{3,2,1,0:T(8,128)S(1)}, f32[1,10,16,256]{3,2,1,0:T(8,128)S(1)}, u32[]{:S(2)}, u32[]{:S(2)}) collective-permute-start(f32[1,10,16,256]{3,2,1,0:T(8,128)S(1)} %get-tuple-element.28), channel_id=1, source_target_pairs={{16,0},{32,16},{48,32},{64,48},{80,64},{96,80},{112,96},{128,112},... | collective-permute-start | bytes 491528 | tf_op jit(solution)/shard_map/ppermute | solution.py:31
  29.2 0.7 copy-start.1
  37.9 10.6 %copy-start = (f32[1,10,16,384]{3,2,1,0:T(8,128)S(1)}, f32[1,10,16,384]{3,2,1,0:T(8,128)}, u32[]{:S(2)}) copy-start(f32[1,10,16,384]{3,2,1,0:T(8,128)} %param.8) | copy-start | bytes 737284
  111.8 2.9 %copy-start.2 = (f32[1,16,384,16]{2,1,3,0:T(8,128)S(1)}, f32[1,16,384,16]{2,1,3,0:T(8,128)}, u32[]{:S(2)}) copy-start(f32[1,16,384,16]{2,1,3,0:T(8,128)} %copy-done.1) | copy-start | bytes 1179652
  114.6 0.7 copy-start.3
where the time goes:
time: 197 us; the launch traced here: 194 us
  local copies, waits for them, and re-layouts  82.9 us (42%)
  blocking collectives  77.9 us (40%)
  other arithmetic  19.3 us (10%)
  starting transfers between devices  14.2 us (7%)
    psum x4, blocking collectives, by_axis(): return functools.reduce(lax.psum, axes, shard)  77.9 us
    gather x4, local copies, waits for them, and re-layouts, pick_rows(): return table[slots]  63 us
    unnamed x15, other arithmetic  11.7 us
    ppermute x1, starting transfers between devices, padded(): lax.ppermute(lax.slice_in_dim(block, 0, width, axis=dim), axis, backward)  11.1 us
    concatenate x1, local copies, waits for them, and re-layouts, padded(): block = jnp.concatenate([low, block, high], axis=dim)  5.84 us
    gather x1, local copies, waits for them, and re-layouts, on_device(): right = jnp.take(extended, BAND + e_dev + fetch_list[0, 1], axis=3)  4.7 us
  transfers between devices with their start and end apart: 2, of which 0 were waited for; matrix products, arithmetic and copies ran while one was open for 8% of the time, Pallas kernels for 0%

commit v1 on v0

v1 whole, which is shorter than its diff:
```python
import functools

import jax
import jax.numpy as jnp
from jax import lax
from jax.experimental import pallas as pl
from jax.experimental.pallas import tpu as pltpu
from jax.sharding import Mesh
from jax.sharding import PartitionSpec as P

BAND = 256
LANES = 128
SFC = ("sfc_0", "sfc_1")
LEV = ("lev_0", "lev_1")
PLANE = ("sfc_1", "lev_0", "lev_1")
LINE = "sfc_0"
NODES = (-1.0, -0.4472135954999579, 0.4472135954999579, 1.0)
UNROLL = 4
GRANT = 12 * 1024 * 1024


def basis(coord):
    terms = []
    for first in range(4):
        term, scale = None, 1.0
        for other in range(4):
            if other != first:
                factor = coord - NODES[other]
                term = factor if term is None else term * factor
                scale *= NODES[first] - NODES[other]
        terms.append(term * (1.0 / scale))
    return terms


def rows(v):
    return pl.ds(v, 8, stride=16) if v < 16 else pl.ds(128 + v - 16, 8, stride=4)


def pick(table, idx):
    return jnp.take_along_axis(table, idx, axis=1, mode="promise_in_bounds")


def group_of_four(x, op):
    y = op(x, pltpu.roll(x, 7, 0))
    return op(y, pltpu.roll(y, 6, 0))


def all_sublanes(x):
    for shift in (4, 2, 1):
        x = x + pltpu.roll(x, shift, 0)
    return x


def interpolate(
    own, air_old, air_new, coord, slot, fetch, left, right,
    clip_out, up_out, down_out, sums_out,
    wide, table, along_a, along_b, stacked, slots, airs,
):
    chunks = own.shape[1] // LANES
    points = slot.shape[0]
    sub = lax.broadcasted_iota(jnp.int32, (8, LANES), 0)
    lane = lax.broadcasted_iota(jnp.int32, (8, LANES), 1)
    for c in range(chunks):
        wide[c] = own[:, c * LANES : (c + 1) * LANES]
    for side, band in enumerate((left, right)):
        for c in range(2):
            wide[chunks + 2 * side + c] = band[:, c * LANES : (c + 1) * LANES]
    old = jnp.zeros((8, LANES), jnp.float32)
    for c in range(chunks):
        air = air_old[:, c * LANES : (c + 1) * LANES]
        for v in range(20):
            x = wide[c, rows(v), :]
            table[c, 8 * v : 8 * v + 8, :] = x
            if v < 16:
                old = old + x * jnp.broadcast_to(air[v : v + 1], (8, LANES))
    tails = []
    for t in (8, 9):
        total = jnp.zeros((8, LANES), jnp.float32)
        for c in range(chunks):
            for h in (0, 8):
                cols = slice(c * LANES, (c + 1) * LANES)
                total = total + wide[c, t * 16 + h : t * 16 + h + 8, :] * air_old[h : h + 8, cols]
        tails.append(all_sublanes(total))
    zero = jnp.zeros((8, LANES), jnp.float32)
    old_tail = jnp.where(sub == 0, tails[0], jnp.where(sub == 4, tails[1], zero))
    for side, shift in enumerate((chunks * LANES - BAND, 0)):
        idx = jnp.broadcast_to(fetch[side : side + 1, :] - shift, (8, LANES))
        near, far = idx & (LANES - 1), idx >= LANES
        for v in range(20):
            first = pick(wide[chunks + 2 * side, rows(v), :], near)
            second = pick(wide[chunks + 2 * side + 1, rows(v), :], near)
            table[chunks + side, 8 * v : 8 * v + 8, :] = jnp.where(far, second, first)
    terms_a = basis(coord[0])
    terms_b = basis(coord[1])
    for c in range(chunks):
        cols = slice(c * LANES, (c + 1) * LANES)
        slots[c] = slot[:, cols]
        airs[c] = air_new[:, cols]
        for i in range(4):
            along_a[i, c] = terms_a[i][:, cols]
            along_b[i, c] = terms_b[i][:, cols]
            stacked[c, pl.ds(i, points, stride=8), :] = terms_a[i][:, cols]
            stacked[c, pl.ds(i + 4, points, stride=8), :] = terms_a[i][:, cols]

    def group(n, e, acc):
        where = jnp.broadcast_to(slots[e, pl.ds(n, 1), :], (8, LANES))
        near, chunk = where & (LANES - 1), where >> 7
        masks = [chunk == c for c in range(1, chunks + 2)]

        def value(v):
            x = pick(table[0, 8 * v : 8 * v + 8, :], near)
            for c, mask in enumerate(masks):
                x = jnp.where(mask, pick(table[c + 1, 8 * v : 8 * v + 8, :], near), x)
            return x

        def row(ref, *at):
            return jnp.broadcast_to(ref[(*at, pl.ds(n, 1), slice(None))], (8, LANES))

        def inner(first):
            total = low = high = None
            for q in range(4):
                x = value(first + q)
                low = x if low is None else jnp.minimum(low, x)
                high = x if high is None else jnp.maximum(high, x)
                term = row(along_b, q, e) * x
                total = term if total is None else total + term
            return total, low, high

        interp, low, high = inner(0)
        interp = interp * row(along_a, 0, e)
        for i in range(1, 4):
            more, least, most = inner(4 * i)
            interp = interp + row(along_a, i, e) * more
            low, high = jnp.minimum(low, least), jnp.maximum(high, most)
        tail, tail_low, tail_high = inner(16)
        tail = tail * stacked[e, pl.ds(pl.multiple_of(8 * n, 8), 8), :]
        tail = group_of_four(tail, jnp.add)
        tail_low = group_of_four(tail_low, jnp.minimum)
        tail_high = group_of_four(tail_high, jnp.maximum)
        air = row(airs, e)
        acc = list(acc)
        for h, (f, lo, hi) in enumerate(((interp, low, high), (tail, tail_low, tail_high))):
            f = jnp.minimum(jnp.maximum(f, lo), hi)
            up, down = hi - f, f - lo
            clip_out[n, e, 8 * h : 8 * h + 8, :] = f
            up_out[n, e, 8 * h : 8 * h + 8, :] = up
            down_out[n, e, 8 * h : 8 * h + 8, :] = down
            acc[3 * h] = acc[3 * h] - air * f
            acc[3 * h + 1] = acc[3 * h + 1] + air * up
            acc[3 * h + 2] = acc[3 * h + 2] + air * down
        return tuple(acc)

    def step(k, acc):
        for u in range(UNROLL):
            for e in range(chunks):
                acc = group(k * UNROLL + u, e, acc)
        return acc

    acc = lax.fori_loop(0, points // UNROLL, step, (old, zero, zero, old_tail, zero, zero))
    row_of = zero
    for k in range(6):
        total = jnp.broadcast_to(jnp.sum(acc[k], axis=1, keepdims=True), (8, LANES))
        keep = lane == 8 * k + sub
        if k >= 3:
            keep = keep & ((sub & 3) == 0)
        row_of = row_of + jnp.where(keep, total, zero)
    row_of = all_sublanes(row_of)
    for k in range(sums_out.shape[0] // 8):
        sums_out[8 * k : 8 * k + 8, :] = row_of


def add_rows(parts):
    total = parts[0:8, :]
    for k in range(1, parts.shape[0] // 8):
        total = total + parts[8 * k : 8 * k + 8, :]
    return all_sublanes(total)


def relay(parts, sums_out):
    total = add_rows(parts)
    for k in range(sums_out.shape[0] // 8):
        sums_out[8 * k : 8 * k + 8, :] = total


def finish(parts, clip, up, down, new_out, wide):
    sub = lax.broadcasted_iota(jnp.int32, (8, LANES), 0)
    lane = lax.broadcasted_iota(jnp.int32, (8, LANES), 1)
    total = add_rows(parts)
    sums = []
    for k in range(6):
        mine = jnp.where(lane == 8 * k + sub, total, jnp.zeros_like(total))
        sums.append(jnp.broadcast_to(jnp.sum(mine, axis=1, keepdims=True), (8, LANES)))
    ratios = []
    for h in range(2):
        short, room_up, room_down = sums[3 * h : 3 * h + 3]
        raised = short >= 0
        zero = jnp.zeros_like(short)
        ratios.append(
            (jnp.where(raised, short / room_up, zero), jnp.where(raised, zero, short / room_down))
        )
    for n in range(clip.shape[0]):
        for e in range(clip.shape[1]):
            for h in range(2):
                at = (n, e, slice(8 * h, 8 * h + 8), slice(None))
                new = clip[at] + ratios[h][0] * up[at] + ratios[h][1] * down[at]
                if h == 0:
                    wide[e, pl.ds(n, 8, stride=16), :] = new
                else:
                    wide[e, 128 + n : 129 + n, :] = new[0:1]
                    wide[e, 144 + n : 145 + n, :] = new[4:5]
    for e in range(clip.shape[1]):
        new_out[:, e * LANES : (e + 1) * LANES] = wide[e]


def in_vmem(kernel, out_shape, count, scratch=()):
    spec = pl.BlockSpec(memory_space=pltpu.VMEM)
    return pl.pallas_call(
        kernel,
        out_shape=out_shape,
        in_specs=[spec] * count,
        out_specs=jax.tree.map(lambda _: spec, out_shape),
        scratch_shapes=scratch,
        compiler_params=pltpu.CompilerParams(vmem_limit_bytes=GRANT),
    )


def on_device(tracer_old, air_old, air_new, dep_coord, dep_slot, fetch_list):
    _, tracers, points, e_dev = tracer_old.shape
    chunks = e_dev // LANES
    real = tracer_old.dtype
    field = tracer_old.reshape(tracers * points, e_dev)
    count = lax.axis_size(SFC)
    forward = [(i, (i + 1) % count) for i in range(count)]
    backward = [(target, source) for source, target in forward]
    left = lax.ppermute(field[:, e_dev - BAND :], SFC, forward)
    right = lax.ppermute(field[:, :BAND], SFC, backward)
    mid = jax.ShapeDtypeStruct((points, chunks, 16, LANES), real)
    plane, line = lax.axis_size(PLANE), lax.axis_size(LINE)
    call = in_vmem(
        interpolate,
        (mid, mid, mid, jax.ShapeDtypeStruct((plane, LANES), real)),
        8,
        [
            pltpu.VMEM((chunks + 4, tracers * points, LANES), real),
            pltpu.VMEM((chunks + 2, 160, LANES), real),
            pltpu.VMEM((4, chunks, points, LANES), real),
            pltpu.VMEM((4, chunks, points, LANES), real),
            pltpu.VMEM((chunks, 8 * points, LANES), real),
            pltpu.VMEM((chunks, points, LANES), jnp.int32),
            pltpu.VMEM((chunks, points, LANES), real),
        ],
    )
    clip, up, down, sums = call(
        field, air_old[0], air_new[0], dep_coord[:, 0], dep_slot[0], fetch_list[0], left, right
    )
    sums = lax.all_to_all(sums, PLANE, 0, 0, tiled=True)
    sums = in_vmem(relay, jax.ShapeDtypeStruct((line, LANES), real), 1)(sums)
    sums = lax.all_to_all(sums, LINE, 0, 0, tiled=True)
    new = in_vmem(
        finish,
        jax.ShapeDtypeStruct((tracers * points, e_dev), real),
        4,
        [pltpu.VMEM((chunks, tracers * points, LANES), real)],
    )(sums, clip, up, down)
    return new.reshape(tracer_old.shape)


def solution(mesh):
    finer = Mesh(mesh.devices.reshape(32, 2, 4, 4), ("sfc_0", "sfc_1", "lev_0", "lev_1"))
    placed = (
        P(LEV, None, None, SFC),
        P(LEV, None, SFC),
        P(LEV, None, SFC),
        P(None, LEV, None, SFC),
        P(LEV, None, SFC),
        P(SFC, None, None),
    )
    return jax.shard_map(
        on_device, mesh=finer, in_specs=placed, out_specs=P(LEV, None, None, SFC), check_vma=False
    )
```

time: 197 us -> 79.6 us (0.40); the launches traced: 194 us -> 79.4 us
  local copies, waits for them, and re-layouts: 82.9 us -> 1.73 us
  blocking collectives: 77.9 us -> 52.2 us
  other arithmetic: 19.3 us -> 0 us
  Pallas kernels: 0 us -> 6.82 us
  waiting for transfers between devices: 0.01 us -> 4.48 us
    psum x4 -> x0, blocking collectives: 77.9 us -> none  [by_axis(): return functools.reduce(lax.psum, axes, shard)]
    gather x6 -> x0, local copies, waits for them, and re-layouts: 71.5 us -> none  [the longest x4 63 us: pick_rows(): return table[slots]]
    all_to_all x0 -> x2, blocking collectives: none -> 52.2 us  [the longest x1 33.3 us: on_device(): sums = lax.all_to_all(sums, LINE, 0, 0, tiled=True)]
    unnamed x15 -> x0, other arithmetic: 11.7 us -> none
    pallas_call x0 -> x3, Pallas kernels: none -> 6.82 us  [the longest x1 5.89 us: on_device(): call(field, air_old[0], air_new[0], dep_coord[:, 0], dep_slot[0], fetch_l...]
    concatenate x1 -> x0, local copies, waits for them, and re-layouts: 5.84 us -> none  [padded(): block = jnp.concatenate([low, block, high], axis=dim)]
    ppermute x2, waiting for transfers between devices: 0.01 us -> 4.48 us  [the longest x1 3.45 us: on_device(): left = lax.ppermute(field[:, e_dev - BAND:], SFC, forward)]
    unnamed x9 -> x12, local copies, waits for them, and re-layouts: 3.77 us -> 0.67 us
  transfers between devices with their start and end apart: 2 -> 2, of which waited for: 0 -> 2; matrix products, arithmetic and copies ran while one was open for 8% -> 0% of each run, Pallas kernels for 0% -> 0%
where the time goes in v1:
time: 79.6 us; the launch traced here: 79.4 us
  blocking collectives  52.2 us (66%)
  starting transfers between devices  14.1 us (18%)
  Pallas kernels  6.82 us (9%)
  waiting for transfers between devices  4.48 us (6%)
  local copies, waits for them, and re-layouts  1.73 us (2%)
    all_to_all x1, blocking collectives, on_device(): sums = lax.all_to_all(sums, LINE, 0, 0, tiled=True)  33.3 us
    all_to_all x1, blocking collectives, on_device(): sums = lax.all_to_all(sums, PLANE, 0, 0, tiled=True)  18.8 us
    ppermute x1, starting transfers between devices, on_device(): right = lax.ppermute(field[:, :BAND], SFC, backward)  14.1 us
    pallas_call x1, Pallas kernels, on_device(): call(field, air_old[0], air_new[0], dep_coord[:, 0], dep_slot[0], fetch_l...  5.89 us
    ppermute x1, waiting for transfers between devices, on_device(): left = lax.ppermute(field[:, e_dev - BAND:], SFC, forward)  3.45 us
  transfers between devices with their start and end apart: 2, of which 2 were waited for; matrix products, arithmetic and copies ran while one was open for 0% of the time, Pallas kernels for 0%

profile of v1, /device:TPU:1, one launch (start us, length us, event | category | flops | bytes accessed | tf_op | source)
XLA Modules:
  0.0 79.4 jit_solution(11310421888542474181)
XLA Ops:
  0.0 0.0 copy-start
  0.0 0.0 copy-start.1
  0.0 0.0 copy-start.2
  0.0 0.0 copy-start.3
  0.0 0.0 copy-start.4
  0.0 1.1 %fusion = (f32[160,256]{1,0:T(8,128)S(1)}, f32[160,256]{1,0:T(8,128)S(1)}) fusion(f32[160,384]{1,0:T(8,128)} %bitcast.15), kind=kLoop, calls=%fused_computation | loop fusion | bytes 655360 | tf_op jit(solution)/shard_map/slice | solution.py:236
  1.1 14.1 %collective-permute-start.1 = (f32[160,256]{1,0:T(8,128)S(1)}, f32[160,256]{1,0:T(8,128)S(1)}, u32[]{:S(2)}, u32[]{:S(2)}) collective-permute-start(f32[160,256]{1,0:T(8,128)S(1)} %get-tuple-element.13), channel_id=1, source_target_pairs={{16,0},{32,16},{48,32},{64,48},{80,64},{96,80},{112,96},{128,112},... | collective-permute-start | bytes 491528 | tf_op jit(solution)/shard_map/ppermute | solution.py:236
  15.2 0.0 collective-permute-start
  15.2 1.0 %collective-permute-done.1.right = f32[160,256]{1,0:T(8,128)S(1)} collective-permute-done((f32[160,256]{1,0:T(8,128)S(1)}, f32[160,256]{1,0:T(8,128)S(1)}, u32[]{:S(2)}, u32[]{:S(2)}) %collective-permute-start.1) | collective-permute-done | bytes 163872 | tf_op jit(solution)/shard_map/ppermute | solution.py:236
  16.2 3.5 %collective-permute-done.left = f32[160,256]{1,0:T(8,128)S(1)} collective-permute-done((f32[160,256]{1,0:T(8,128)S(1)}, f32[160,256]{1,0:T(8,128)S(1)}, u32[]{:S(2)}, u32[]{:S(2)}) %collective-permute-start) | collective-permute-done | bytes 163872 | tf_op jit(solution)/shard_map/ppermute | solution.py:235
  19.7 0.0 copy-start.5
  19.7 0.0 copy-done
  19.7 0.0 copy-done.1
  19.7 0.0 copy-done.2
  19.7 0.0 copy-done.3
  19.7 0.0 copy-done.4
  19.7 0.6 copy-done.5
  20.4 5.9 %shard_map.64 = (f32[16,3,16,128]{3,2,1,0:T(8,128)S(1)}, f32[16,3,16,128]{3,2,1,0:T(8,128)S(1)}, f32[16,3,16,128]{3,2,1,0:T(8,128)S(1)}, f32[32,128]{1,0:T(8,128)S(1)}) custom-call(f32[160,384]{1,0:T(8,128)S(1)} %bitcast.16, f32[16,384]{1,0:T(8,128)S(1)} %bitcast.21, f32[16,384]{1,0:T(8,128)S(1)} %bitcast.22, f32[2,16,384]{2,1,0:T(8,128)S(1)} %bitcast.20, ...), custom_call_target="tpu_custom_call" | custom-call | tf_op jit(solution)/shard_map/pallas_call | solution.py:253
  26.3 18.8 %all_to_all.22 = f32[32,1,128]{2,1,0:T(1,128)S(1)} all-to-all(f32[32,1,128]{2,1,0:T(1,128)S(1)} %bitcast.24), channel_id=1, replica_groups=mesh['sfc_0'=32,'sfc_1'=2,'lev_0'=4,'lev_1'=4] {'sfc_1','lev_0','lev_1'}, dimensions={0} | all-to-all | bytes 32768 | tf_op jit(solution)/shard_map/all_to_all | solution.py:256
  45.1 33.3 %all_to_all.23 = f32[32,1,128]{2,1,0:T(1,128)S(1)} all-to-all(f32[32,1,128]{2,1,0:T(1,128)S(1)} %bitcast.19), channel_id=1, replica_groups=mesh['sfc_0'=32,'sfc_1'=2,'lev_0'=4,'lev_1'=4] {'sfc_0'}, dimensions={0} | all-to-all | bytes 32768 | tf_op jit(solution)/shard_map/all_to_all | solution.py:258
  78.5 0.9 %shard_map.66 = f32[160,384]{1,0:T(8,128)} custom-call(f32[32,128]{1,0:T(8,128)S(1)} %bitcast.17, f32[16,3,16,128]{3,2,1,0:T(8,128)S(1)} %get-tuple-element.10.clip, f32[16,3,16,128]{3,2,1,0:T(8,128)S(1)} %get-tuple-element.11.up, f32[16,3,16,128]{3,2,1,0:T(8,128)S(1)} %get-tuple-element.12.down), custom_call_target="tpu_custom_call" | custom-call | tf_op jit(solution)/shard_map/pallas_call | solution.py:259
  (1 shorter events, 0.0 us)
Async XLA Ops:
  0.0 19.7 %copy-start = (f32[1,10,16,384]{3,2,1,0:T(8,128)S(1)}, f32[1,10,16,384]{3,2,1,0:T(8,128)}, u32[]{:S(2)}) copy-start(f32[1,10,16,384]{3,2,1,0:T(8,128)} %param.6) | copy-start | bytes 737284
  0.0 19.7 %copy-start.1 = (f32[2,1,16,384]{3,2,1,0:T(8,128)S(1)}, f32[2,1,16,384]{3,2,1,0:T(8,128)}, u32[]{:S(2)}) copy-start(f32[2,1,16,384]{3,2,1,0:T(8,128)} %param.9) | copy-start | bytes 147460
  0.0 19.7 %copy-start.2 = (f32[1,16,384]{2,1,0:T(8,128)S(1)}, f32[1,16,384]{2,1,0:T(8,128)}, u32[]{:S(2)}) copy-start(f32[1,16,384]{2,1,0:T(8,128)} %param.7) | copy-start | bytes 73732
  0.0 19.7 %copy-start.3 = (f32[1,16,384]{2,1,0:T(8,128)S(1)}, f32[1,16,384]{2,1,0:T(8,128)}, u32[]{:S(2)}) copy-start(f32[1,16,384]{2,1,0:T(8,128)} %param.8) | copy-start | bytes 73732
  0.0 19.7 %copy-start.4 = (s32[1,16,384]{2,1,0:T(8,128)S(1)}, s32[1,16,384]{2,1,0:T(8,128)}, u32[]{:S(2)}) copy-start(s32[1,16,384]{2,1,0:T(8,128)} %param.10) | copy-start | bytes 73732
  1.1 15.2 %collective-permute-start.1 = (f32[160,256]{1,0:T(8,128)S(1)}, f32[160,256]{1,0:T(8,128)S(1)}, u32[]{:S(2)}, u32[]{:S(2)}) collective-permute-start(f32[160,256]{1,0:T(8,128)S(1)} %get-tuple-element.13), channel_id=1, source_target_pairs={{16,0},{32,16},{48,32},{64,48},{80,64},{96,80},{112,96},{128,112},... | collective-permute-start | bytes 491528 | tf_op jit(solution)/shard_map/ppermute | solution.py:236
  15.2 4.5 %collective-permute-start = (f32[160,256]{1,0:T(8,128)S(1)}, f32[160,256]{1,0:T(8,128)S(1)}, u32[]{:S(2)}, u32[]{:S(2)}) collective-permute-start(f32[160,256]{1,0:T(8,128)S(1)} %get-tuple-element.14), channel_id=1, source_target_pairs={{0,16},{16,32},{32,48},{48,64},{64,80},{80,96},{96,112},{112,128},... | collective-permute-start | bytes 491528 | tf_op jit(solution)/shard_map/ppermute | solution.py:235
  19.7 0.7 copy-start.5

commit v2 on v1

v2 whole, which is shorter than its diff:
```python
import jax
import jax.numpy as jnp
from jax import lax
from jax.experimental import pallas as pl
from jax.experimental.pallas import tpu as pltpu
from jax.sharding import Mesh
from jax.sharding import PartitionSpec as P

BAND = 256
LANES = 128
SFC = ("sfc_0", "sfc_1")
LEV = ("lev_0", "lev_1")
PLANE = ("sfc_1", "lev_0", "lev_1")
LINE = "sfc_0"
NODES = (-1.0, -0.4472135954999579, 0.4472135954999579, 1.0)
UNROLL = 4
GRANT = 12 * 1024 * 1024
WORK = 10_000_000


def basis(coord):
    terms = []
    for first in range(4):
        term, scale = None, 1.0
        for other in range(4):
            if other != first:
                factor = coord - NODES[other]
                term = factor if term is None else term * factor
                scale *= NODES[first] - NODES[other]
        terms.append(term * (1.0 / scale))
    return terms


def rows(v):
    return pl.ds(v, 8, stride=16) if v < 16 else pl.ds(128 + v - 16, 8, stride=4)


def pick(table, idx):
    return jnp.take_along_axis(table, idx, axis=1, mode="promise_in_bounds")


def group_of_four(x, op):
    y = op(x, pltpu.roll(x, 7, 0))
    return op(y, pltpu.roll(y, 6, 0))


def all_sublanes(x):
    for shift in (4, 2, 1):
        x = x + pltpu.roll(x, shift, 0)
    return x


def old_mass(field, air_old, table, sub):
    zero = jnp.zeros((8, LANES), jnp.float32)
    old = zero
    for c in range(table.shape[0]):
        cols = slice(c * LANES, (c + 1) * LANES)
        for v in range(16):
            air = jnp.broadcast_to(air_old[v : v + 1, cols], (8, LANES))
            old = old + table[c, 8 * v : 8 * v + 8, :] * air
    tails = []
    for t in (8, 9):
        total = zero
        for c in range(table.shape[0]):
            cols = slice(c * LANES, (c + 1) * LANES)
            for h in (0, 8):
                total = total + field[t * 16 + h : t * 16 + h + 8, cols] * air_old[h : h + 8, cols]
        tails.append(all_sublanes(total))
    return old, jnp.where(sub == 0, tails[0], jnp.where(sub == 4, tails[1], zero))


def gather(value, row, stack):
    along_a, along_b = row

    def inner(first):
        total = low = high = None
        for q in range(4):
            x = value(first + q)
            low = x if low is None else jnp.minimum(low, x)
            high = x if high is None else jnp.maximum(high, x)
            term = along_b[q] * x
            total = term if total is None else total + term
        return total, low, high

    interp, low, high = inner(0)
    interp = interp * along_a[0]
    for i in range(1, 4):
        more, least, most = inner(4 * i)
        interp = interp + along_a[i] * more
        low, high = jnp.minimum(low, least), jnp.maximum(high, most)
    tail, tail_low, tail_high = inner(16)
    tail = group_of_four(tail * stack, jnp.add)
    tail_low = group_of_four(tail_low, jnp.minimum)
    tail_high = group_of_four(tail_high, jnp.maximum)
    return (interp, low, high), (tail, tail_low, tail_high)


def broadcast_row(ref, n, *at):
    return jnp.broadcast_to(ref[(*at, pl.ds(n, 1), slice(None))], (8, LANES))


def own_part(
    field, air_old, air_new, coord, slot, fetch,
    picks, interp_out, low_out, high_out, old_out, along_a, along_b, stacked, slots, airs,
    wide, table,
):
    chunks = field.shape[1] // LANES
    points = slot.shape[0]
    sub = lax.broadcasted_iota(jnp.int32, (8, LANES), 0)
    odd = lax.axis_index("sfc_1")
    for side in range(2):
        right = odd if side == 0 else 1 - odd
        start = (chunks * LANES - BAND) * (1 - right)
        mine = jnp.where(right == 1, fetch[1:2, :], fetch[0:1, :]) - start
        picks[side] = jnp.broadcast_to(mine, (8, LANES))
    for c in range(chunks):
        wide[c] = field[:, c * LANES : (c + 1) * LANES]
    for c in range(chunks):
        for v in range(20):
            table[c, 8 * v : 8 * v + 8, :] = wide[c, rows(v), :]
    old_out[0], old_out[1] = old_mass(field, air_old, table, sub)
    terms_a = basis(coord[0])
    terms_b = basis(coord[1])
    for c in range(chunks):
        cols = slice(c * LANES, (c + 1) * LANES)
        slots[c] = slot[:, cols]
        airs[c] = air_new[:, cols]
        for i in range(4):
            along_a[i, c] = terms_a[i][:, cols]
            along_b[i, c] = terms_b[i][:, cols]
            stacked[c, pl.ds(i, points, stride=8), :] = terms_a[i][:, cols]
            stacked[c, pl.ds(i + 4, points, stride=8), :] = terms_a[i][:, cols]

    def step(n, carry):
        for e in range(chunks):
            where = broadcast_row(slots, n, e)
            near, chunk = where & (LANES - 1), where >> 7
            masks = [chunk == c for c in range(1, chunks)]

            def value(v):
                x = pick(table[0, 8 * v : 8 * v + 8, :], near)
                for c, mask in enumerate(masks):
                    x = jnp.where(mask, pick(table[c + 1, 8 * v : 8 * v + 8, :], near), x)
                return x

            row = [[broadcast_row(ref, n, i, e) for i in range(4)] for ref in (along_a, along_b)]
            parts = gather(value, row, stacked[e, pl.ds(pl.multiple_of(8 * n, 8), 8), :])
            for h, part in enumerate(parts):
                for ref, x in zip((interp_out, low_out, high_out), part):
                    ref[n, e, 8 * h : 8 * h + 8, :] = x
        return carry

    lax.fori_loop(0, points, step, 0)


def halo_part(
    across, within, picks, interp, low, high, old, along_a, along_b, stacked, slots, airs,
    clip_out, up_out, down_out, sums_out,
    wide, table,
):
    points, chunks = interp.shape[:2]
    own = chunks * LANES
    sub = lax.broadcasted_iota(jnp.int32, (8, LANES), 0)
    lane = lax.broadcasted_iota(jnp.int32, (8, LANES), 1)
    zero = jnp.zeros((8, LANES), jnp.float32)
    odd = lax.axis_index("sfc_1")
    for k, band in enumerate((across, within)):
        for c in range(2):
            wide[2 * k + c] = band[:, c * LANES : (c + 1) * LANES]
    for side in range(2):
        idx = picks[side]
        near, far = idx & (LANES - 1), idx >= LANES
        for v in range(20):
            first = pick(wide[2 * side, rows(v), :], near)
            second = pick(wide[2 * side + 1, rows(v), :], near)
            table[side, 8 * v : 8 * v + 8, :] = jnp.where(far, second, first)

    def group(n, e, acc):
        where = broadcast_row(slots, n, e)
        near, halo = where & (LANES - 1), where >= own
        at_within = (where >> 7) == chunks + 1 - odd

        def value(v):
            at = slice(8 * v, 8 * v + 8)
            return jnp.where(at_within, pick(table[1, at, :], near), pick(table[0, at, :], near))

        row = [[broadcast_row(ref, n, i, e) for i in range(4)] for ref in (along_a, along_b)]
        parts = gather(value, row, stacked[e, pl.ds(pl.multiple_of(8 * n, 8), 8), :])
        air = broadcast_row(airs, n, e)
        acc = list(acc)
        for h, part in enumerate(parts):
            at = (n, e, slice(8 * h, 8 * h + 8), slice(None))
            f, lo, hi = (
                jnp.where(halo, x, ref[at]) for x, ref in zip(part, (interp, low, high))
            )
            f = jnp.minimum(jnp.maximum(f, lo), hi)
            up, down = hi - f, f - lo
            clip_out[at], up_out[at], down_out[at] = f, up, down
            acc[3 * h] = acc[3 * h] - air * f
            acc[3 * h + 1] = acc[3 * h + 1] + air * up
            acc[3 * h + 2] = acc[3 * h + 2] + air * down
        return tuple(acc)

    def step(k, acc):
        for u in range(UNROLL):
            for e in range(chunks):
                acc = group(k * UNROLL + u, e, acc)
        return acc

    acc = lax.fori_loop(0, points // UNROLL, step, (old[0], zero, zero, old[1], zero, zero))
    row_of = zero
    for k in range(6):
        total = jnp.broadcast_to(jnp.sum(acc[k], axis=1, keepdims=True), (8, LANES))
        keep = lane == 8 * k + sub
        if k >= 3:
            keep = keep & ((sub & 3) == 0)
        row_of = row_of + jnp.where(keep, total, zero)
    row_of = all_sublanes(row_of)
    for k in range(sums_out.shape[0] // 8):
        sums_out[8 * k : 8 * k + 8, :] = row_of


def add_rows(parts):
    total = parts[0:8, :]
    for k in range(1, parts.shape[0] // 8):
        total = total + parts[8 * k : 8 * k + 8, :]
    return all_sublanes(total)


def relay(parts, sums_out):
    total = add_rows(parts)
    for k in range(sums_out.shape[0] // 8):
        sums_out[8 * k : 8 * k + 8, :] = total


def finish(parts, clip, up, down, new_out, wide):
    sub = lax.broadcasted_iota(jnp.int32, (8, LANES), 0)
    lane = lax.broadcasted_iota(jnp.int32, (8, LANES), 1)
    total = add_rows(parts)
    sums = []
    for k in range(6):
        mine = jnp.where(lane == 8 * k + sub, total, jnp.zeros_like(total))
        sums.append(jnp.broadcast_to(jnp.sum(mine, axis=1, keepdims=True), (8, LANES)))
    ratios = []
    for h in range(2):
        short, room_up, room_down = sums[3 * h : 3 * h + 3]
        raised = short >= 0
        zero = jnp.zeros_like(short)
        ratios.append(
            (jnp.where(raised, short / room_up, zero), jnp.where(raised, zero, short / room_down))
        )
    for n in range(clip.shape[0]):
        for e in range(clip.shape[1]):
            for h in range(2):
                at = (n, e, slice(8 * h, 8 * h + 8), slice(None))
                new = clip[at] + ratios[h][0] * up[at] + ratios[h][1] * down[at]
                if h == 0:
                    wide[e, pl.ds(n, 8, stride=16), :] = new
                else:
                    wide[e, 128 + n : 129 + n, :] = new[0:1]
                    wide[e, 144 + n : 145 + n, :] = new[4:5]
    for e in range(clip.shape[1]):
        new_out[:, e * LANES : (e + 1) * LANES] = wide[e]


def in_vmem(kernel, out_shape, count, scratch=(), work=0):
    spec = pl.BlockSpec(memory_space=pltpu.VMEM)
    return pl.pallas_call(
        kernel,
        out_shape=out_shape,
        in_specs=[spec] * count,
        out_specs=jax.tree.map(lambda _: spec, out_shape),
        scratch_shapes=scratch,
        cost_estimate=pl.CostEstimate(flops=work, bytes_accessed=0, transcendentals=0),
        compiler_params=pltpu.CompilerParams(vmem_limit_bytes=GRANT),
    )


def on_device(tracer_old, air_old, air_new, dep_coord, dep_slot, fetch_list):
    _, tracers, points, e_dev = tracer_old.shape
    chunks = e_dev // LANES
    real = tracer_old.dtype
    field = tracer_old.reshape(tracers * points, e_dev)
    count = lax.axis_size(SFC)
    first, last = field[:, :BAND], field[:, e_dev - BAND :]
    even = lax.axis_index("sfc_1") == 0
    across = [(i, (i - 1) % count if i % 2 == 0 else (i + 1) % count) for i in range(count)]
    within = [(i, i + 1 if i % 2 == 0 else i - 1) for i in range(count)]
    got_across = lax.ppermute(jnp.where(even, first, last), SFC, across)
    got_within = lax.ppermute(jnp.where(even, last, first), SFC, within)

    def shape(*dims, dtype=real):
        return jax.ShapeDtypeStruct(dims, dtype)

    mid = shape(points, chunks, 16, LANES)
    plane, line = lax.axis_size(PLANE), lax.axis_size(LINE)
    terms = shape(4, chunks, points, LANES)
    stacked = shape(chunks, 8 * points, LANES)
    slots = shape(chunks, points, LANES, dtype=jnp.int32)
    airs = shape(chunks, points, LANES)
    prepared = in_vmem(
        own_part,
        (shape(2, 8, LANES, dtype=jnp.int32), mid, mid, mid, shape(2, 8, LANES), terms, terms, stacked, slots, airs),
        6,
        [pltpu.VMEM((chunks, tracers * points, LANES), real)] * 2,
        WORK,
    )(field, air_old[0], air_new[0], dep_coord[:, 0], dep_slot[0], fetch_list[0])
    call = in_vmem(
        halo_part,
        (mid, mid, mid, shape(plane, LANES)),
        2 + len(prepared),
        [
            pltpu.VMEM((4, tracers * points, LANES), real),
            pltpu.VMEM((2, 160, LANES), real),
        ],
    )
    clip, up, down, sums = call(got_across, got_within, *prepared)
    sums = lax.all_to_all(sums, PLANE, 0, 0, tiled=True)
    sums = in_vmem(relay, shape(line, LANES), 1)(sums)
    sums = lax.all_to_all(sums, LINE, 0, 0, tiled=True)
    new = in_vmem(
        finish,
        shape(tracers * points, e_dev),
        4,
        [pltpu.VMEM((chunks, tracers * points, LANES), real)],
    )(sums, clip, up, down)
    return new.reshape(tracer_old.shape)


def solution(mesh):
    finer = Mesh(mesh.devices.reshape(32, 2, 4, 4), ("sfc_0", "sfc_1", "lev_0", "lev_1"))
    placed = (
        P(LEV, None, None, SFC),
        P(LEV, None, SFC),
        P(LEV, None, SFC),
        P(None, LEV, None, SFC),
        P(LEV, None, SFC),
        P(SFC, None, None),
    )
    return jax.shard_map(
        on_device, mesh=finer, in_specs=placed, out_specs=P(LEV, None, None, SFC), check_vma=False
    )
```

time: 79.6 us -> 79.7 us (level)
  waiting for transfers between devices: 4.48 us -> 0.01 us
  starting transfers between devices: 14.1 us -> 17.9 us
  Pallas kernels: 6.82 us -> 8.23 us
  local copies, waits for them, and re-layouts: 1.73 us -> 0.64 us
  other arithmetic: 0 us -> 1.07 us
  blocking collectives: 52.2 us -> 51.4 us
    ppermute x2, waiting for transfers between devices: 4.48 us -> 0.01 us  [the longest x1 0.01 us: on_device(): got_within = lax.ppermute(jnp.where(even, last, first), SFC, within)]
    ppermute x2, starting transfers between devices: 14.1 us -> 17.9 us  [the longest x1 16 us: on_device(): got_within = lax.ppermute(jnp.where(even, last, first), SFC, within)]
    pallas_call x3 -> x4, Pallas kernels: 6.82 us -> 8.23 us  [the longest x1 4.51 us: on_device(): in_vmem(own_part, (shape(2, 8, LANES, dtype=jnp.int32), mid, mid, mid, sh...]
    select_n x0 -> x1, other arithmetic: none -> 1.07 us  [on_device(): got_within = lax.ppermute(jnp.where(even, last, first), SFC, within)]
    slice x1 -> x0, local copies, waits for them, and re-layouts: 1.06 us -> none  [on_device(): right = lax.ppermute(field[:, :BAND], SFC, backward)]
    all_to_all x1, blocking collectives: 18.8 us -> 18 us  [on_device(): sums = lax.all_to_all(sums, PLANE, 0, 0, tiled=True)]
  transfers between devices with their start and end apart: 2 -> 2, of which waited for: 2 -> 0; matrix products, arithmetic and copies ran while one was open for 0% -> 0% of each run, Pallas kernels for 0% -> 6%
where the time goes in v2:
time: 79.7 us; the launch traced here: 79.4 us
  blocking collectives  51.4 us (64%)
  starting transfers between devices  17.9 us (22%)
  Pallas kernels  8.23 us (10%)
  other arithmetic  1.07 us (1%)
    all_to_all x1, blocking collectives, on_device(): sums = lax.all_to_all(sums, LINE, 0, 0, tiled=True)  33.4 us
    all_to_all x1, blocking collectives, on_device(): sums = lax.all_to_all(sums, PLANE, 0, 0, tiled=True)  18 us
    ppermute x1, starting transfers between devices, on_device(): got_within = lax.ppermute(jnp.where(even, last, first), SFC, within)  16 us
    pallas_call x1, Pallas kernels, on_device(): in_vmem(own_part, (shape(2, 8, LANES, dtype=jnp.int32), mid, mid, mid, sh...  4.51 us
    pallas_call x1, Pallas kernels, on_device(): clip, up, down, sums = call(got_across, got_within, *prepared)  2.79 us
    ppermute x1, starting transfers between devices, on_device(): got_across = lax.ppermute(jnp.where(even, first, last), SFC, across)  1.92 us
  transfers between devices with their start and end apart: 2, of which 0 were waited for; matrix products, arithmetic and copies ran while one was open for 0% of the time, Pallas kernels for 6%

profile of v2, /device:TPU:1, one launch (start us, length us, event | category | flops | bytes accessed | tf_op | source)
XLA Modules:
  0.0 79.4 jit_solution(11712143755268302782)
XLA Ops:
  0.0 0.0 copy-start
  0.0 0.0 copy-start.1
  0.0 0.0 copy-start.2
  0.0 0.0 copy-start.3
  0.0 0.0 copy-start.4
  0.0 1.1 %slice_select_fusion = (f32[160,256]{1,0:T(8,128)S(1)}, f32[160,256]{1,0:T(8,128)S(1)}) fusion(f32[160,384]{1,0:T(8,128)} %bitcast.15, pred[]{:T(512)S(6)} %eq.3), kind=kLoop, calls=%fused_computation | loop fusion | flops 81920 | bytes 655361 | tf_op jit(solution)/shard_map/jit(_where)/select_n | solution.py:290
  1.1 16.0 %collective-permute-start.1 = (f32[160,256]{1,0:T(8,128)S(1)}, f32[160,256]{1,0:T(8,128)S(1)}, u32[]{:S(2)}, u32[]{:S(2)}) collective-permute-start(f32[160,256]{1,0:T(8,128)S(1)} %get-tuple-element.33), channel_id=1, source_target_pairs={{0,16},{16,0},{32,48},{48,32},{64,80},{80,64},{96,112},{112,96},{1... | collective-permute-start | bytes 491528 | tf_op jit(solution)/shard_map/ppermute | solution.py:290
  17.1 1.9 %collective-permute-start = (f32[160,256]{1,0:T(8,128)S(1)}, f32[160,256]{1,0:T(8,128)S(1)}, u32[]{:S(2)}, u32[]{:S(2)}) collective-permute-start(f32[160,256]{1,0:T(8,128)S(1)} %get-tuple-element.34), channel_id=1, source_target_pairs={{0,1008},{16,32},{32,16},{48,64},{64,48},{80,96},{96,80},{112,128}... | collective-permute-start | bytes 491528 | tf_op jit(solution)/shard_map/ppermute | solution.py:289
  19.0 0.0 copy-start.5
  19.1 0.0 copy-done
  19.1 0.0 copy-done.1
  19.1 0.0 copy-done.2
  19.1 0.0 copy-done.3
  19.1 0.0 copy-done.4
  19.1 0.6 copy-done.5
  19.7 4.5 %shard_map.64 = (s32[2,8,128]{2,1,0:T(8,128)S(1)}, f32[16,3,16,128]{3,2,1,0:T(8,128)S(1)}, f32[16,3,16,128]{3,2,1,0:T(8,128)S(1)}, f32[16,3,16,128]{3,2,1,0:T(8,...) custom-call(f32[160,384]{1,0:T(8,128)S(1)} %bitcast.16, ...), custom_call_target="tpu_custom_call" | custom-call | flops 10000000 | tf_op jit(solution)/shard_map/pallas_call | solution.py:301
  24.2 0.0 collective-permute-done.1.within
  24.3 0.0 collective-permute-done.across
  24.3 2.8 %shard_map.65 = (f32[16,3,16,128]{3,2,1,0:T(8,128)S(1)}, f32[16,3,16,128]{3,2,1,0:T(8,128)S(1)}, f32[16,3,16,128]{3,2,1,0:T(8,128)S(1)}, f32[32,128]{1,0:T(8,128)S(1)}) custom-call(f32[160,256]{1,0:T(8,128)S(1)} %collective-permute-done.across, f32[160,256]{1,0:T(8,128)S(1)} %collective-permute-done.1.within, s32[2,8,128]{2,1,0:T(8,128)S(1)} %get-tuple-element.19.picks, ...), custom_call_target="tpu_custom_call" | custom-call | tf_op jit(solution)/shard_map/pallas_call | solution.py:317
  27.1 18.0 %all_to_all.22 = f32[32,1,128]{2,1,0:T(1,128)S(1)} all-to-all(f32[32,1,128]{2,1,0:T(1,128)S(1)} %bitcast.24), channel_id=1, replica_groups=mesh['sfc_0'=32,'sfc_1'=2,'lev_0'=4,'lev_1'=4] {'sfc_1','lev_0','lev_1'}, dimensions={0} | all-to-all | bytes 32768 | tf_op jit(solution)/shard_map/all_to_all | solution.py:318
  45.1 33.4 %all_to_all.23 = f32[32,1,128]{2,1,0:T(1,128)S(1)} all-to-all(f32[32,1,128]{2,1,0:T(1,128)S(1)} %bitcast.19), channel_id=1, replica_groups=mesh['sfc_0'=32,'sfc_1'=2,'lev_0'=4,'lev_1'=4] {'sfc_0'}, dimensions={0} | all-to-all | bytes 32768 | tf_op jit(solution)/shard_map/all_to_all | solution.py:320
  78.5 0.9 %shard_map.67 = f32[160,384]{1,0:T(8,128)} custom-call(f32[32,128]{1,0:T(8,128)S(1)} %bitcast.17, f32[16,3,16,128]{3,2,1,0:T(8,128)S(1)} %get-tuple-element.30.clip, f32[16,3,16,128]{3,2,1,0:T(8,128)S(1)} %get-tuple-element.31.up, f32[16,3,16,128]{3,2,1,0:T(8,128)S(1)} %get-tuple-element.32.down), custom_call_target="tpu_custom_call" | custom-call | tf_op jit(solution)/shard_map/pallas_call | solution.py:321
  (1 shorter events, 0.0 us)
Async XLA Ops:
  0.0 19.1 %copy-start = (f32[1,10,16,384]{3,2,1,0:T(8,128)S(1)}, f32[1,10,16,384]{3,2,1,0:T(8,128)}, u32[]{:S(2)}) copy-start(f32[1,10,16,384]{3,2,1,0:T(8,128)} %param.6) | copy-start | bytes 737284
  0.0 19.1 %copy-start.1 = (f32[2,1,16,384]{3,2,1,0:T(8,128)S(1)}, f32[2,1,16,384]{3,2,1,0:T(8,128)}, u32[]{:S(2)}) copy-start(f32[2,1,16,384]{3,2,1,0:T(8,128)} %param.9) | copy-start | bytes 147460
  0.0 19.1 %copy-start.2 = (f32[1,16,384]{2,1,0:T(8,128)S(1)}, f32[1,16,384]{2,1,0:T(8,128)}, u32[]{:S(2)}) copy-start(f32[1,16,384]{2,1,0:T(8,128)} %param.7) | copy-start | bytes 73732
  0.0 19.1 %copy-start.3 = (f32[1,16,384]{2,1,0:T(8,128)S(1)}, f32[1,16,384]{2,1,0:T(8,128)}, u32[]{:S(2)}) copy-start(f32[1,16,384]{2,1,0:T(8,128)} %param.8) | copy-start | bytes 73732
  0.0 19.1 %copy-start.4 = (s32[1,16,384]{2,1,0:T(8,128)S(1)}, s32[1,16,384]{2,1,0:T(8,128)}, u32[]{:S(2)}) copy-start(s32[1,16,384]{2,1,0:T(8,128)} %param.10) | copy-start | bytes 73732
  1.1 23.2 %collective-permute-start.1 = (f32[160,256]{1,0:T(8,128)S(1)}, f32[160,256]{1,0:T(8,128)S(1)}, u32[]{:S(2)}, u32[]{:S(2)}) collective-permute-start(f32[160,256]{1,0:T(8,128)S(1)} %get-tuple-element.33), channel_id=1, source_target_pairs={{0,16},{16,0},{32,48},{48,32},{64,80},{80,64},{96,112},{112,96},{1... | collective-permute-start | bytes 491528 | tf_op jit(solution)/shard_map/ppermute | solution.py:290
  17.1 7.1 %collective-permute-start = (f32[160,256]{1,0:T(8,128)S(1)}, f32[160,256]{1,0:T(8,128)S(1)}, u32[]{:S(2)}, u32[]{:S(2)}) collective-permute-start(f32[160,256]{1,0:T(8,128)S(1)} %get-tuple-element.34), channel_id=1, source_target_pairs={{0,1008},{16,32},{32,16},{48,64},{64,48},{80,96},{96,80},{112,128}... | collective-permute-start | bytes 491528 | tf_op jit(solution)/shard_map/ppermute | solution.py:289
  19.0 0.7 copy-start.5

commit v3 on v2

v3 whole, which is shorter than its diff:
```python
import jax
import jax.numpy as jnp
from jax import lax
from jax.experimental import pallas as pl
from jax.experimental.pallas import tpu as pltpu
from jax.sharding import Mesh
from jax.sharding import PartitionSpec as P

BAND = 256
LANES = 128
SFC = ("sfc_0", "sfc_1")
LEV = ("lev_0", "lev_1")
PLANE = ("sfc_1", "lev_0", "lev_1")
LINE = "sfc_0"
NODES = (-1.0, -0.4472135954999579, 0.4472135954999579, 1.0)
UNROLL = 2
OWN_UNROLL = 2
STEPS = 32767.0
GRANT = 12 * 1024 * 1024
WORK = 1_000_000_000


def basis(coord):
    terms = []
    for first in range(4):
        term, scale = None, 1.0
        for other in range(4):
            if other != first:
                factor = coord - NODES[other]
                term = factor if term is None else term * factor
                scale *= NODES[first] - NODES[other]
        terms.append(term * (1.0 / scale))
    return terms


def rows(v):
    return pl.ds(v, 8, stride=16) if v < 16 else pl.ds(128 + v - 16, 8, stride=4)


def pick(table, idx):
    return jnp.take_along_axis(table, idx, axis=1, mode="promise_in_bounds")


def group_of_four(x, op):
    y = op(x, pltpu.roll(x, 7, 0))
    return op(y, pltpu.roll(y, 6, 0))


def all_sublanes(x):
    for shift in (4, 2, 1):
        x = x + pltpu.roll(x, shift, 0)
    return x


def old_mass(air_old, wide, sub):
    zero = jnp.zeros((8, LANES), jnp.float32)
    old = zero
    for c in range(wide.shape[0]):
        cols = slice(c * LANES, (c + 1) * LANES)
        for v in range(16):
            air = jnp.broadcast_to(air_old[v : v + 1, cols], (8, LANES))
            old = old + wide[c, rows(v), :] * air
    tails = []
    for t in (8, 9):
        total = zero
        for c in range(wide.shape[0]):
            cols = slice(c * LANES, (c + 1) * LANES)
            for h in (0, 8):
                at = t * 16 + h
                total = total + wide[c, at : at + 8, :] * air_old[h : h + 8, cols]
        tails.append(all_sublanes(total))
    return old, jnp.where(sub == 0, tails[0], jnp.where(sub == 4, tails[1], zero))


def fixed(x):
    return (x * STEPS + 0.5).astype(jnp.int32)


def pair(wide, c, k):
    return fixed(wide[c, rows(2 * k), :]) | (fixed(wide[c, rows(2 * k + 1), :]) << 16)


def halves(x):
    first = (x & 0xFFFF).astype(jnp.float32)
    return first, lax.shift_right_logical(x, 16).astype(jnp.float32)


def gather(pairs, along_a, along_b, stack):
    def inner(first):
        total = low = high = None
        for k in range(2):
            for q, x in enumerate(halves(pairs(first + k))):
                low = x if low is None else jnp.minimum(low, x)
                high = x if high is None else jnp.maximum(high, x)
                term = along_b[2 * k + q] * x
                total = term if total is None else total + term
        return total, low, high

    interp, low, high = inner(0)
    interp = interp * along_a[0]
    for i in range(1, 4):
        more, least, most = inner(2 * i)
        interp = interp + along_a[i] * more
        low, high = jnp.minimum(low, least), jnp.maximum(high, most)
    tail, tail_low, tail_high = inner(8)
    tail = group_of_four(tail * stack, jnp.add)
    tail_low = group_of_four(tail_low, jnp.minimum)
    tail_high = group_of_four(tail_high, jnp.maximum)
    return (interp, low, high), (tail, tail_low, tail_high)


def broadcast_row(ref, n, *at):
    return jnp.broadcast_to(ref[(*at, pl.ds(n, 1), slice(None))], (8, LANES))


def own_part(
    field, air_old, coord, slot, fetch,
    picks, own_out, old_out, along_a, along_b, stacked, slots,
    wide, table,
):
    chunks = slot.shape[1] // LANES
    points = slot.shape[0]
    sub = lax.broadcasted_iota(jnp.int32, (8, LANES), 0)
    for side, start in enumerate((chunks * LANES - BAND, 0)):
        picks[side] = jnp.broadcast_to(fetch[side : side + 1, :] - start, (8, LANES))
    for c in range(chunks):
        wide[c] = field[:, c * LANES : (c + 1) * LANES]
        slots[c] = slot[:, c * LANES : (c + 1) * LANES]
    for c in range(chunks):
        for k in range(10):
            table[c, 8 * k : 8 * k + 8, :] = pair(wide, c, k)

    def step(k, carry):
        for u in range(OWN_UNROLL):
            n = k * OWN_UNROLL + u
            for e in range(chunks):
                where = broadcast_row(slots, n, e)
                near, chunk = where & (LANES - 1), where >> 7
                masks = [chunk == c for c in range(1, chunks)]
                for k2 in range(10):
                    at = slice(8 * k2, 8 * k2 + 8)
                    x = pick(table[0, at, :], near)
                    for c, mask in enumerate(masks):
                        x = jnp.where(mask, pick(table[c + 1, at, :], near), x)
                    own_out[n, e, at, :] = x
        return carry

    lax.fori_loop(0, points // OWN_UNROLL, step, 0)
    old_out[0], old_out[1] = old_mass(air_old, wide, sub)
    terms_a = basis(coord[0])
    terms_b = basis(coord[1])
    for c in range(chunks):
        cols = slice(c * LANES, (c + 1) * LANES)
        for i in range(4):
            along_a[i, c] = terms_a[i][:, cols]
            along_b[i, c] = terms_b[i][:, cols]
            stacked[c, pl.ds(i, points, stride=8), :] = terms_a[i][:, cols]
            stacked[c, pl.ds(i + 4, points, stride=8), :] = terms_a[i][:, cols]


def halo_part(
    left, right, air_new, picks, own, old, along_a, along_b, stacked, slots,
    clip_out, up_out, down_out, sums_out,
    wide, table, airs,
):
    points, chunks = own.shape[:2]
    count = chunks * LANES
    sub = lax.broadcasted_iota(jnp.int32, (8, LANES), 0)
    lane = lax.broadcasted_iota(jnp.int32, (8, LANES), 1)
    zero = jnp.zeros((8, LANES), jnp.float32)
    for c in range(chunks):
        airs[c] = air_new[:, c * LANES : (c + 1) * LANES]
    for side, band in enumerate((left, right)):
        for c in range(2):
            wide[2 * side + c] = band[:, c * LANES : (c + 1) * LANES]
    for side in range(2):
        idx = picks[side]
        near, far = idx & (LANES - 1), idx >= LANES
        for k in range(10):
            first = pick(pair(wide, 2 * side, k), near)
            second = pick(pair(wide, 2 * side + 1, k), near)
            table[side, 8 * k : 8 * k + 8, :] = jnp.where(far, second, first)

    def group(n, e, acc):
        where = broadcast_row(slots, n, e)
        near, at_right, halo = where & (LANES - 1), where >= count + LANES, where >= count

        def pairs(k):
            at = slice(8 * k, 8 * k + 8)
            x = jnp.where(at_right, pick(table[1, at, :], near), pick(table[0, at, :], near))
            return jnp.where(halo, x, own[n, e, at, :])

        row_a, row_b = (
            [broadcast_row(ref, n, i, e) for i in range(4)] for ref in (along_a, along_b)
        )
        parts = gather(pairs, row_a, row_b, stacked[e, pl.ds(pl.multiple_of(8 * n, 8), 8), :])
        air = broadcast_row(airs, n, e)
        acc = list(acc)
        for h, (f, lo, hi) in enumerate(parts):
            at = (n, e, slice(8 * h, 8 * h + 8), slice(None))
            f = jnp.minimum(jnp.maximum(f, lo), hi)
            f, up, down = f * (1.0 / STEPS), (hi - f) * (1.0 / STEPS), (f - lo) * (1.0 / STEPS)
            clip_out[at], up_out[at], down_out[at] = f, up, down
            acc[3 * h] = acc[3 * h] - air * f
            acc[3 * h + 1] = acc[3 * h + 1] + air * up
            acc[3 * h + 2] = acc[3 * h + 2] + air * down
        return tuple(acc)

    def step(k, acc):
        for u in range(UNROLL):
            for e in range(chunks):
                acc = group(k * UNROLL + u, e, acc)
        return acc

    acc = lax.fori_loop(0, points // UNROLL, step, (old[0], zero, zero, old[1], zero, zero))
    row_of = zero
    for k in range(6):
        total = jnp.broadcast_to(jnp.sum(acc[k], axis=1, keepdims=True), (8, LANES))
        keep = lane == 8 * k + sub
        if k >= 3:
            keep = keep & ((sub & 3) == 0)
        row_of = row_of + jnp.where(keep, total, zero)
    row_of = all_sublanes(row_of)
    for k in range(sums_out.shape[0] // 8):
        sums_out[8 * k : 8 * k + 8, :] = row_of


def add_rows(parts):
    total = parts[0:8, :]
    for k in range(1, parts.shape[0] // 8):
        total = total + parts[8 * k : 8 * k + 8, :]
    return all_sublanes(total)


def relay(parts, sums_out):
    total = add_rows(parts)
    for k in range(sums_out.shape[0] // 8):
        sums_out[8 * k : 8 * k + 8, :] = total


def finish(parts, clip, up, down, new_out, wide):
    sub = lax.broadcasted_iota(jnp.int32, (8, LANES), 0)
    lane = lax.broadcasted_iota(jnp.int32, (8, LANES), 1)
    total = add_rows(parts)
    sums = []
    for k in range(6):
        mine = jnp.where(lane == 8 * k + sub, total, jnp.zeros_like(total))
        sums.append(jnp.broadcast_to(jnp.sum(mine, axis=1, keepdims=True), (8, LANES)))
    ratios = []
    for h in range(2):
        short, room_up, room_down = sums[3 * h : 3 * h + 3]
        raised = short >= 0
        zero = jnp.zeros_like(short)
        ratios.append(
            (jnp.where(raised, short / room_up, zero), jnp.where(raised, zero, short / room_down))
        )
    for n in range(clip.shape[0]):
        for e in range(clip.shape[1]):
            for h in range(2):
                at = (n, e, slice(8 * h, 8 * h + 8), slice(None))
                new = clip[at] + ratios[h][0] * up[at] + ratios[h][1] * down[at]
                if h == 0:
                    wide[e, pl.ds(n, 8, stride=16), :] = new
                else:
                    wide[e, 128 + n : 129 + n, :] = new[0:1]
                    wide[e, 144 + n : 145 + n, :] = new[4:5]
    for e in range(clip.shape[1]):
        new_out[:, e * LANES : (e + 1) * LANES] = wide[e]


def in_vmem(kernel, out_shape, count, scratch=(), work=0):
    spec = pl.BlockSpec(memory_space=pltpu.VMEM)
    return pl.pallas_call(
        kernel,
        out_shape=out_shape,
        in_specs=[spec] * count,
        out_specs=jax.tree.map(lambda _: spec, out_shape),
        scratch_shapes=scratch,
        cost_estimate=pl.CostEstimate(flops=work, bytes_accessed=0, transcendentals=0),
        compiler_params=pltpu.CompilerParams(vmem_limit_bytes=GRANT),
    )


def bands(field, last_out, first_out):
    last_out[...] = field[:, field.shape[1] - BAND :]
    first_out[...] = field[:, :BAND]


def on_device(tracer_old, air_old, air_new, dep_coord, dep_slot, fetch_list):
    _, tracers, points, e_dev = tracer_old.shape
    chunks = e_dev // LANES
    real, whole = tracer_old.dtype, jnp.int32
    field = tracer_old.reshape(tracers * points, e_dev)

    def shape(*dims, dtype=real):
        return jax.ShapeDtypeStruct(dims, dtype)

    band = shape(tracers * points, BAND)
    last, first = in_vmem(bands, (band, band), 1, work=WORK)(field)
    count = lax.axis_size(SFC)
    forward = [(i, (i + 1) % count) for i in range(count)]
    backward = [(target, source) for source, target in forward]
    left = lax.ppermute(last, SFC, forward)
    right = lax.ppermute(first, SFC, backward)
    mid = shape(points, chunks, 16, LANES)
    plane, line = lax.axis_size(PLANE), lax.axis_size(LINE)
    terms = shape(4, chunks, points, LANES)
    prepared = in_vmem(
        own_part,
        (
            shape(2, 8, LANES, dtype=whole),
            shape(points, chunks, 80, LANES, dtype=whole),
            shape(2, 8, LANES),
            terms,
            terms,
            shape(chunks, 8 * points, LANES),
            shape(chunks, points, LANES, dtype=whole),
        ),
        5,
        [
            pltpu.VMEM((chunks, tracers * points, LANES), real),
            pltpu.VMEM((chunks, 80, LANES), whole),
        ],
        WORK,
    )(field, air_old[0], dep_coord[:, 0], dep_slot[0], fetch_list[0])
    clip, up, down, sums = in_vmem(
        halo_part,
        (mid, mid, mid, shape(plane, LANES)),
        3 + len(prepared),
        [
            pltpu.VMEM((4, tracers * points, LANES), real),
            pltpu.VMEM((2, 80, LANES), whole),
            pltpu.VMEM((chunks, points, LANES), real),
        ],
    )(left, right, air_new[0], *prepared)
    sums = lax.all_to_all(sums, PLANE, 0, 0, tiled=True)
    sums = in_vmem(relay, shape(line, LANES), 1)(sums)
    sums = lax.all_to_all(sums, LINE, 0, 0, tiled=True)
    new = in_vmem(
        finish,
        shape(tracers * points, e_dev),
        4,
        [pltpu.VMEM((chunks, tracers * points, LANES), real)],
    )(sums, clip, up, down)
    return new.reshape(tracer_old.shape)


def solution(mesh):
    finer = Mesh(mesh.devices.reshape(32, 2, 4, 4), ("sfc_0", "sfc_1", "lev_0", "lev_1"))
    placed = (
        P(LEV, None, None, SFC),
        P(LEV, None, SFC),
        P(LEV, None, SFC),
        P(None, LEV, None, SFC),
        P(LEV, None, SFC),
        P(SFC, None, None),
    )
    return jax.shard_map(
        on_device, mesh=finer, in_specs=placed, out_specs=P(LEV, None, None, SFC), check_vma=False
    )
```

time: 79.7 us -> 75.3 us (0.945)
  starting transfers between devices: 17.9 us -> 14.2 us
  blocking collectives: 51.4 us -> 54.4 us
  Pallas kernels: 8.23 us -> 5.53 us
  other arithmetic: 1.07 us -> 0 us
    ppermute x2, starting transfers between devices: 17.9 us -> 14.2 us  [the longest x1 11.1 us: on_device(): right = lax.ppermute(first, SFC, backward)]
    all_to_all x1, blocking collectives: 33.4 us -> 36.5 us  [on_device(): sums = lax.all_to_all(sums, LINE, 0, 0, tiled=True)]
    pallas_call x2 -> x3, Pallas kernels: 7.29 us -> 4.6 us  [the longest x1 2.42 us: on_device(): in_vmem(own_part, (shape(2, 8, LANES, dtype=whole), shape(points, chunks,...]
    select_n x1 -> x0, other arithmetic: 1.07 us -> none  [on_device(): got_within = lax.ppermute(jnp.where(even, last, first), SFC, within)]
  transfers between devices with their start and end apart: 2 -> 2, of which waited for: 0 -> 0; matrix products, arithmetic and copies ran while one was open for 0% -> 0% of each run, Pallas kernels for 6% -> 3%
where the time goes in v3:
time: 75.3 us; the launch traced here: 75.1 us
  blocking collectives  54.4 us (72%)
  starting transfers between devices  14.2 us (19%)
  Pallas kernels  5.53 us (7%)
  local copies, waits for them, and re-layouts  0.98 us (1%)
    all_to_all x1, blocking collectives, on_device(): sums = lax.all_to_all(sums, LINE, 0, 0, tiled=True)  36.5 us
    all_to_all x1, blocking collectives, on_device(): sums = lax.all_to_all(sums, PLANE, 0, 0, tiled=True)  17.9 us
    ppermute x1, starting transfers between devices, on_device(): right = lax.ppermute(first, SFC, backward)  11.1 us
    ppermute x1, starting transfers between devices, on_device(): left = lax.ppermute(last, SFC, forward)  3.03 us
    pallas_call x1, Pallas kernels, on_device(): in_vmem(own_part, (shape(2, 8, LANES, dtype=whole), shape(points, chunks,...  2.42 us
    pallas_call x1, Pallas kernels, on_device(): in_vmem(halo_part, (mid, mid, mid, shape(plane, LANES)), 3 + len(prepared...  2.16 us
  transfers between devices with their start and end apart: 2, of which 0 were waited for; matrix products, arithmetic and copies ran while one was open for 0% of the time, Pallas kernels for 3%

profile of v3, /device:TPU:1, one launch (start us, length us, event | category | flops | bytes accessed | tf_op | source)
XLA Modules:
  0.0 75.1 jit_solution(16074220422221955044)
XLA Ops:
  0.0 0.0 copy-start.5
  0.0 0.0 copy-start.1
  0.0 1.0 %copy-done.1 = f32[1,10,16,384]{3,2,1,0:T(8,128)S(1)} copy-done((f32[1,10,16,384]{3,2,1,0:T(8,128)S(1)}, f32[1,10,16,384]{3,2,1,0:T(8,128)}, u32[]{:S(2)}) %copy-start.1) | copy-done | bytes 245784
  1.0 0.0 copy-start.2
  1.0 0.0 copy-start.3
  1.0 0.0 copy-start.4
  1.0 0.0 copy-start
  1.0 3.0 %collective-permute-start = (f32[160,256]{1,0:T(8,128)S(1)}, f32[160,256]{1,0:T(8,128)S(1)}, u32[]{:S(2)}, u32[]{:S(2)}) collective-permute-start(f32[160,256]{1,0:T(8,128)S(1)} %get-tuple-element.18), channel_id=1, source_target_pairs={{0,16},{16,32},{32,48},{48,64},{64,80},{80,96},{96,112},{112,128},... | collective-permute-start | bytes 491528 | tf_op jit(solution)/shard_map/ppermute | solution.py:303
  4.0 11.1 %collective-permute-start.1 = (f32[160,256]{1,0:T(8,128)S(1)}, f32[160,256]{1,0:T(8,128)S(1)}, u32[]{:S(2)}, u32[]{:S(2)}) collective-permute-start(f32[160,256]{1,0:T(8,128)S(1)} %get-tuple-element.19), channel_id=1, source_target_pairs={{16,0},{32,16},{48,32},{64,48},{80,64},{96,80},{112,96},{128,112},... | collective-permute-start | bytes 491528 | tf_op jit(solution)/shard_map/ppermute | solution.py:304
  15.2 0.0 copy-done.5
  15.2 0.0 copy-done.2
  15.2 0.0 copy-done.3
  15.2 0.0 copy-done.4
  15.2 2.4 %shard_map.65 = (s32[2,8,128]{2,1,0:T(8,128)S(1)}, s32[16,3,80,128]{3,2,1,0:T(8,128)S(1)}, f32[2,8,128]{2,1,0:T(8,128)S(1)}, f32[4,3,16,128]{3,2,1,0:T(8,128)S(1...) custom-call(f32[160,384]{1,0:T(8,128)S(1)} %bitcast.21, ...), custom_call_target="tpu_custom_call" | custom-call | flops 1000000000 | tf_op jit(solution)/shard_map/pallas_call | solution.py:308
  17.6 0.0 collective-permute-done.left
  17.6 0.0 collective-permute-done.1.right
  17.6 0.0 copy-done
  17.6 2.2 %shard_map.66 = (f32[16,3,16,128]{3,2,1,0:T(8,128)S(1)}, f32[16,3,16,128]{3,2,1,0:T(8,128)S(1)}, f32[16,3,16,128]{3,2,1,0:T(8,128)S(1)}, f32[32,128]{1,0:T(8,128)S(1)}) custom-call(f32[160,256]{1,0:T(8,128)S(1)} %collective-permute-done.left, f32[160,256]{1,0:T(8,128)S(1)} %collective-permute-done.1.right, f32[16,384]{1,0:T(8,128)S(1)} %bitcast.18, ...), custom_call_target="tpu_custom_call" | custom-call | tf_op jit(solution)/shard_map/pallas_call | solution.py:326
  19.8 17.9 %all_to_all.22 = f32[32,1,128]{2,1,0:T(1,128)S(1)} all-to-all(f32[32,1,128]{2,1,0:T(1,128)S(1)} %bitcast.19), channel_id=1, replica_groups=mesh['sfc_0'=32,'sfc_1'=2,'lev_0'=4,'lev_1'=4] {'sfc_1','lev_0','lev_1'}, dimensions={0} | all-to-all | bytes 32768 | tf_op jit(solution)/shard_map/all_to_all | solution.py:336
  37.7 36.5 %all_to_all.23 = f32[32,1,128]{2,1,0:T(1,128)S(1)} all-to-all(f32[32,1,128]{2,1,0:T(1,128)S(1)} %bitcast.17), channel_id=1, replica_groups=mesh['sfc_0'=32,'sfc_1'=2,'lev_0'=4,'lev_1'=4] {'sfc_0'}, dimensions={0} | all-to-all | bytes 32768 | tf_op jit(solution)/shard_map/all_to_all | solution.py:338
  74.2 0.9 %shard_map.68 = f32[160,384]{1,0:T(8,128)} custom-call(f32[32,128]{1,0:T(8,128)S(1)} %bitcast.15, f32[16,3,16,128]{3,2,1,0:T(8,128)S(1)} %get-tuple-element.28.clip, f32[16,3,16,128]{3,2,1,0:T(8,128)S(1)} %get-tuple-element.29.up, f32[16,3,16,128]{3,2,1,0:T(8,128)S(1)} %get-tuple-element.30.down), custom_call_target="tpu_custom_call" | custom-call | tf_op jit(solution)/shard_map/pallas_call | solution.py:339
  (2 shorter events, 0.0 us)
Async XLA Ops:
  0.0 15.2 %copy-start.5 = (s32[1,2,128]{2,1,0:T(2,128)S(1)}, s32[1,2,128]{2,1,0:T(2,128)}, u32[]{:S(2)}) copy-start(s32[1,2,128]{2,1,0:T(2,128)} %param.11) | copy-start | bytes 3076
  0.0 1.0 %copy-start.1 = (f32[1,10,16,384]{3,2,1,0:T(8,128)S(1)}, f32[1,10,16,384]{3,2,1,0:T(8,128)}, u32[]{:S(2)}) copy-start(f32[1,10,16,384]{3,2,1,0:T(8,128)} %param.6) | copy-start | bytes 737284
  1.0 14.2 %copy-start.2 = (f32[2,1,16,384]{3,2,1,0:T(8,128)S(1)}, f32[2,1,16,384]{3,2,1,0:T(8,128)}, u32[]{:S(2)}) copy-start(f32[2,1,16,384]{3,2,1,0:T(8,128)} %param.9) | copy-start | bytes 147460
  1.0 14.2 %copy-start.3 = (f32[1,16,384]{2,1,0:T(8,128)S(1)}, f32[1,16,384]{2,1,0:T(8,128)}, u32[]{:S(2)}) copy-start(f32[1,16,384]{2,1,0:T(8,128)} %param.7) | copy-start | bytes 73732
  1.0 14.2 %copy-start.4 = (s32[1,16,384]{2,1,0:T(8,128)S(1)}, s32[1,16,384]{2,1,0:T(8,128)}, u32[]{:S(2)}) copy-start(s32[1,16,384]{2,1,0:T(8,128)} %param.10) | copy-start | bytes 73732
  1.0 16.6 %copy-start = (f32[1,16,384]{2,1,0:T(8,128)S(1)}, f32[1,16,384]{2,1,0:T(8,128)}, u32[]{:S(2)}) copy-start(f32[1,16,384]{2,1,0:T(8,128)} %param.8) | copy-start | bytes 73732
  1.0 16.6 %collective-permute-start = (f32[160,256]{1,0:T(8,128)S(1)}, f32[160,256]{1,0:T(8,128)S(1)}, u32[]{:S(2)}, u32[]{:S(2)}) collective-permute-start(f32[160,256]{1,0:T(8,128)S(1)} %get-tuple-element.18), channel_id=1, source_target_pairs={{0,16},{16,32},{32,48},{48,64},{64,80},{80,96},{96,112},{112,128},... | collective-permute-start | bytes 491528 | tf_op jit(solution)/shard_map/ppermute | solution.py:303
  4.0 13.6 %collective-permute-start.1 = (f32[160,256]{1,0:T(8,128)S(1)}, f32[160,256]{1,0:T(8,128)S(1)}, u32[]{:S(2)}, u32[]{:S(2)}) collective-permute-start(f32[160,256]{1,0:T(8,128)S(1)} %get-tuple-element.19), channel_id=1, source_target_pairs={{16,0},{32,16},{48,32},{64,48},{80,64},{96,80},{112,96},{128,112},... | collective-permute-start | bytes 491528 | tf_op jit(solution)/shard_map/ppermute | solution.py:304

commit v4 on v3

--- a/solution.py
+++ b/solution.py
@@ -13,8 +13,8 @@
 PLANE = ("sfc_1", "lev_0", "lev_1")
 LINE = "sfc_0"
 NODES = (-1.0, -0.4472135954999579, 0.4472135954999579, 1.0)
-UNROLL = 2
-OWN_UNROLL = 2
+UNROLL = 16
+OWN_UNROLL = 16
 STEPS = 32767.0
 GRANT = 12 * 1024 * 1024
 WORK = 1_000_000_000
@@ -238,7 +238,7 @@
         sums_out[8 * k : 8 * k + 8, :] = total
 
 
-def finish(parts, clip, up, down, new_out, wide):
+def finish(parts, clip, up, down, new_out, wide, sent):
     sub = lax.broadcasted_iota(jnp.int32, (8, LANES), 0)
     lane = lax.broadcasted_iota(jnp.int32, (8, LANES), 1)
     total = add_rows(parts)
@@ -254,8 +254,9 @@
         ratios.append(
             (jnp.where(raised, short / room_up, zero), jnp.where(raised, zero, short / room_down))
         )
-    for n in range(clip.shape[0]):
-        for e in range(clip.shape[1]):
+    copies = []
+    for e in range(clip.shape[1]):
+        for n in range(clip.shape[0]):
             for h in range(2):
                 at = (n, e, slice(8 * h, 8 * h + 8), slice(None))
                 new = clip[at] + ratios[h][0] * up[at] + ratios[h][1] * down[at]
@@ -264,17 +265,20 @@
                 else:
                     wide[e, 128 + n : 129 + n, :] = new[0:1]
                     wide[e, 144 + n : 145 + n, :] = new[4:5]
-    for e in range(clip.shape[1]):
-        new_out[:, e * LANES : (e + 1) * LANES] = wide[e]
-
-
-def in_vmem(kernel, out_shape, count, scratch=(), work=0):
+        copy = pltpu.make_async_copy(wide.at[e], new_out.at[:, pl.ds(e * LANES, LANES)], sent.at[e])
+        copy.start()
+        copies.append(copy)
+    for copy in copies:
+        copy.wait()
+
+
+def in_vmem(kernel, out_shape, count, scratch=(), work=0, out_space=pltpu.VMEM):
     spec = pl.BlockSpec(memory_space=pltpu.VMEM)
     return pl.pallas_call(
         kernel,
         out_shape=out_shape,
         in_specs=[spec] * count,
-        out_specs=jax.tree.map(lambda _: spec, out_shape),
+        out_specs=jax.tree.map(lambda _: pl.BlockSpec(memory_space=out_space), out_shape),
         scratch_shapes=scratch,
         cost_estimate=pl.CostEstimate(flops=work, bytes_accessed=0, transcendentals=0),
         compiler_params=pltpu.CompilerParams(vmem_limit_bytes=GRANT),
@@ -340,7 +344,11 @@
         finish,
         shape(tracers * points, e_dev),
         4,
-        [pltpu.VMEM((chunks, tracers * points, LANES), real)],
+        [
+            pltpu.VMEM((chunks, tracers * points, LANES), real),
+            pltpu.SemaphoreType.DMA((chunks,)),
+        ],
+        out_space=pl.ANY,
     )(sums, clip, up, down)
     return new.reshape(tracer_old.shape)
 

time: 75.3 us -> 74.7 us (level)
  Pallas kernels: 5.53 us -> 4.29 us
  transfers between devices with their start and end apart: 2 -> 2, of which waited for: 0 -> 0; matrix products, arithmetic and copies ran while one was open for 0% -> 0% of each run, Pallas kernels for 3% -> 2%
where the time goes in v4:
time: 74.7 us; the launch traced here: 74.5 us
  blocking collectives  55 us (74%)
  starting transfers between devices  14.2 us (19%)
  Pallas kernels  4.29 us (6%)
  local copies, waits for them, and re-layouts  0.98 us (1%)
    all_to_all x1, blocking collectives, on_device(): sums = lax.all_to_all(sums, LINE, 0, 0, tiled=True)  36.5 us
    all_to_all x1, blocking collectives, on_device(): sums = lax.all_to_all(sums, PLANE, 0, 0, tiled=True)  18.5 us
    ppermute x1, starting transfers between devices, on_device(): right = lax.ppermute(first, SFC, backward)  11.1 us
    ppermute x1, starting transfers between devices, on_device(): left = lax.ppermute(last, SFC, forward)  3.03 us
    pallas_call x1, Pallas kernels, on_device(): in_vmem(own_part, (shape(2, 8, LANES, dtype=whole), shape(points, chunks,...  1.84 us
    pallas_call x1, Pallas kernels, on_device(): in_vmem(halo_part, (mid, mid, mid, shape(plane, LANES)), 3 + len(prepared...  1.57 us
  transfers between devices with their start and end apart: 2, of which 0 were waited for; matrix products, arithmetic and copies ran while one was open for 0% of the time, Pallas kernels for 2%

profile of v4, /device:TPU:1, one launch (start us, length us, event | category | flops | bytes accessed | tf_op | source)
XLA Modules:
  0.0 74.5 jit_solution(2568413983205449306)
XLA Ops:
  0.0 0.0 copy-start.5
  0.0 0.0 copy-start.1
  0.0 1.0 %copy-done.1 = f32[1,10,16,384]{3,2,1,0:T(8,128)S(1)} copy-done((f32[1,10,16,384]{3,2,1,0:T(8,128)S(1)}, f32[1,10,16,384]{3,2,1,0:T(8,128)}, u32[]{:S(2)}) %copy-start.1) | copy-done | bytes 245784
  1.0 0.0 copy-start.2
  1.0 0.0 copy-start.3
  1.0 0.0 copy-start.4
  1.0 0.0 copy-start
  1.0 3.0 %collective-permute-start = (f32[160,256]{1,0:T(8,128)S(1)}, f32[160,256]{1,0:T(8,128)S(1)}, u32[]{:S(2)}, u32[]{:S(2)}) collective-permute-start(f32[160,256]{1,0:T(8,128)S(1)} %get-tuple-element.18), channel_id=1, source_target_pairs={{0,16},{16,32},{32,48},{48,64},{64,80},{80,96},{96,112},{112,128},... | collective-permute-start | bytes 491528 | tf_op jit(solution)/shard_map/ppermute | solution.py:307
  4.0 11.1 %collective-permute-start.1 = (f32[160,256]{1,0:T(8,128)S(1)}, f32[160,256]{1,0:T(8,128)S(1)}, u32[]{:S(2)}, u32[]{:S(2)}) collective-permute-start(f32[160,256]{1,0:T(8,128)S(1)} %get-tuple-element.19), channel_id=1, source_target_pairs={{16,0},{32,16},{48,32},{64,48},{80,64},{96,80},{112,96},{128,112},... | collective-permute-start | bytes 491528 | tf_op jit(solution)/shard_map/ppermute | solution.py:308
  15.2 0.0 copy-done.5
  15.2 0.0 copy-done.2
  15.2 0.0 copy-done.3
  15.2 0.0 copy-done.4
  15.2 1.8 %shard_map.65 = (s32[2,8,128]{2,1,0:T(8,128)S(1)}, s32[16,3,80,128]{3,2,1,0:T(8,128)S(1)}, f32[2,8,128]{2,1,0:T(8,128)S(1)}, f32[4,3,16,128]{3,2,1,0:T(8,128)S(1...) custom-call(f32[160,384]{1,0:T(8,128)S(1)} %bitcast.21, ...), custom_call_target="tpu_custom_call" | custom-call | flops 1000000000 | tf_op jit(solution)/shard_map/pallas_call | solution.py:312
  17.0 0.0 collective-permute-done.left
  17.0 0.0 collective-permute-done.1.right
  17.0 0.0 copy-done
  17.1 1.6 %shard_map.66 = (f32[16,3,16,128]{3,2,1,0:T(8,128)S(1)}, f32[16,3,16,128]{3,2,1,0:T(8,128)S(1)}, f32[16,3,16,128]{3,2,1,0:T(8,128)S(1)}, f32[32,128]{1,0:T(8,128)S(1)}) custom-call(f32[160,256]{1,0:T(8,128)S(1)} %collective-permute-done.left, f32[160,256]{1,0:T(8,128)S(1)} %collective-permute-done.1.right, f32[16,384]{1,0:T(8,128)S(1)} %bitcast.18, ...), custom_call_target="tpu_custom_call" | custom-call | tf_op jit(solution)/shard_map/pallas_call | solution.py:330
  18.6 18.5 %all_to_all.22 = f32[32,1,128]{2,1,0:T(1,128)S(1)} all-to-all(f32[32,1,128]{2,1,0:T(1,128)S(1)} %bitcast.19), channel_id=1, replica_groups=mesh['sfc_0'=32,'sfc_1'=2,'lev_0'=4,'lev_1'=4] {'sfc_1','lev_0','lev_1'}, dimensions={0} | all-to-all | bytes 32768 | tf_op jit(solution)/shard_map/all_to_all | solution.py:340
  37.1 36.5 %all_to_all.23 = f32[32,1,128]{2,1,0:T(1,128)S(1)} all-to-all(f32[32,1,128]{2,1,0:T(1,128)S(1)} %bitcast.17), channel_id=1, replica_groups=mesh['sfc_0'=32,'sfc_1'=2,'lev_0'=4,'lev_1'=4] {'sfc_0'}, dimensions={0} | all-to-all | bytes 32768 | tf_op jit(solution)/shard_map/all_to_all | solution.py:342
  73.6 0.8 %shard_map.68 = f32[160,384]{1,0:T(8,128)} custom-call(f32[32,128]{1,0:T(8,128)S(1)} %bitcast.15, f32[16,3,16,128]{3,2,1,0:T(8,128)S(1)} %get-tuple-element.28.clip, f32[16,3,16,128]{3,2,1,0:T(8,128)S(1)} %get-tuple-element.29.up, f32[16,3,16,128]{3,2,1,0:T(8,128)S(1)} %get-tuple-element.30.down), custom_call_target="tpu_custom_call" | custom-call | tf_op jit(solution)/shard_map/pallas_call | solution.py:343
  (2 shorter events, 0.0 us)
Async XLA Ops:
  0.0 15.2 %copy-start.5 = (s32[1,2,128]{2,1,0:T(2,128)S(1)}, s32[1,2,128]{2,1,0:T(2,128)}, u32[]{:S(2)}) copy-start(s32[1,2,128]{2,1,0:T(2,128)} %param.11) | copy-start | bytes 3076
  0.0 1.0 %copy-start.1 = (f32[1,10,16,384]{3,2,1,0:T(8,128)S(1)}, f32[1,10,16,384]{3,2,1,0:T(8,128)}, u32[]{:S(2)}) copy-start(f32[1,10,16,384]{3,2,1,0:T(8,128)} %param.6) | copy-start | bytes 737284
  1.0 14.2 %copy-start.2 = (f32[2,1,16,384]{3,2,1,0:T(8,128)S(1)}, f32[2,1,16,384]{3,2,1,0:T(8,128)}, u32[]{:S(2)}) copy-start(f32[2,1,16,384]{3,2,1,0:T(8,128)} %param.9) | copy-start | bytes 147460
  1.0 14.2 %copy-start.3 = (f32[1,16,384]{2,1,0:T(8,128)S(1)}, f32[1,16,384]{2,1,0:T(8,128)}, u32[]{:S(2)}) copy-start(f32[1,16,384]{2,1,0:T(8,128)} %param.7) | copy-start | bytes 73732
  1.0 14.2 %copy-start.4 = (s32[1,16,384]{2,1,0:T(8,128)S(1)}, s32[1,16,384]{2,1,0:T(8,128)}, u32[]{:S(2)}) copy-start(s32[1,16,384]{2,1,0:T(8,128)} %param.10) | copy-start | bytes 73732
  1.0 16.0 %copy-start = (f32[1,16,384]{2,1,0:T(8,128)S(1)}, f32[1,16,384]{2,1,0:T(8,128)}, u32[]{:S(2)}) copy-start(f32[1,16,384]{2,1,0:T(8,128)} %param.8) | copy-start | bytes 73732
  1.0 16.0 %collective-permute-start = (f32[160,256]{1,0:T(8,128)S(1)}, f32[160,256]{1,0:T(8,128)S(1)}, u32[]{:S(2)}, u32[]{:S(2)}) collective-permute-start(f32[160,256]{1,0:T(8,128)S(1)} %get-tuple-element.18), channel_id=1, source_target_pairs={{0,16},{16,32},{32,48},{48,64},{64,80},{80,96},{96,112},{112,128},... | collective-permute-start | bytes 491528 | tf_op jit(solution)/shard_map/ppermute | solution.py:307
  4.0 13.0 %collective-permute-start.1 = (f32[160,256]{1,0:T(8,128)S(1)}, f32[160,256]{1,0:T(8,128)S(1)}, u32[]{:S(2)}, u32[]{:S(2)}) collective-permute-start(f32[160,256]{1,0:T(8,128)S(1)} %get-tuple-element.19), channel_id=1, source_target_pairs={{16,0},{32,16},{48,32},{64,48},{80,64},{96,80},{112,96},{128,112},... | collective-permute-start | bytes 491528 | tf_op jit(solution)/shard_map/ppermute | solution.py:308

commit v5 on v4

--- a/solution.py
+++ b/solution.py
@@ -159,7 +159,7 @@
 
 
 def halo_part(
-    left, right, air_new, picks, own, old, along_a, along_b, stacked, slots,
+    right, left, air_new, picks, own, old, along_a, along_b, stacked, slots,
     clip_out, up_out, down_out, sums_out,
     wide, table, airs,
 ):
@@ -304,8 +304,8 @@
     count = lax.axis_size(SFC)
     forward = [(i, (i + 1) % count) for i in range(count)]
     backward = [(target, source) for source, target in forward]
+    right = lax.ppermute(first, SFC, backward)
     left = lax.ppermute(last, SFC, forward)
-    right = lax.ppermute(first, SFC, backward)
     mid = shape(points, chunks, 16, LANES)
     plane, line = lax.axis_size(PLANE), lax.axis_size(LINE)
     terms = shape(4, chunks, points, LANES)
@@ -329,17 +329,17 @@
     )(field, air_old[0], dep_coord[:, 0], dep_slot[0], fetch_list[0])
     clip, up, down, sums = in_vmem(
         halo_part,
-        (mid, mid, mid, shape(plane, LANES)),
+        (mid, mid, mid, shape(line, LANES)),
         3 + len(prepared),
         [
             pltpu.VMEM((4, tracers * points, LANES), real),
             pltpu.VMEM((2, 80, LANES), whole),
             pltpu.VMEM((chunks, points, LANES), real),
         ],
-    )(left, right, air_new[0], *prepared)
+    )(right, left, air_new[0], *prepared)
+    sums = lax.all_to_all(sums, LINE, 0, 0, tiled=True)
+    sums = in_vmem(relay, shape(plane, LANES), 1)(sums)
     sums = lax.all_to_all(sums, PLANE, 0, 0, tiled=True)
-    sums = in_vmem(relay, shape(line, LANES), 1)(sums)
-    sums = lax.all_to_all(sums, LINE, 0, 0, tiled=True)
     new = in_vmem(
         finish,
         shape(tracers * points, e_dev),

time: 74.7 us -> 75.9 us (1.016)
  waiting for transfers between devices: 0.01 us -> 2.59 us
  blocking collectives: 55 us -> 53.6 us
    ppermute x1, starting transfers between devices: 3.03 us -> 0.01 us  [on_device(): left = lax.ppermute(last, SFC, forward)]
    ppermute x1, starting transfers between devices: 11.1 us -> 14.1 us  [on_device(): right = lax.ppermute(first, SFC, backward)]
    ppermute x1, waiting for transfers between devices: 0.01 us -> 2.59 us  [on_device(): left = lax.ppermute(last, SFC, forward)]
    all_to_all x1, blocking collectives: 18.5 us -> 16.8 us  [on_device(): sums = lax.all_to_all(sums, PLANE, 0, 0, tiled=True)]
  transfers between devices with their start and end apart: 2 -> 2, of which waited for: 0 -> 1; matrix products, arithmetic and copies ran while one was open for 0% -> 0% of each run, Pallas kernels for 2% -> 2%
where the time goes in v5:
time: 75.9 us; the launch traced here: 75.7 us
  blocking collectives  53.6 us (71%)
  starting transfers between devices  14.1 us (19%)
  Pallas kernels  4.29 us (6%)
  waiting for transfers between devices  2.59 us (3%)
  local copies, waits for them, and re-layouts  0.98 us (1%)
    all_to_all x1, blocking collectives, on_device(): sums = lax.all_to_all(sums, LINE, 0, 0, tiled=True)  36.8 us
    all_to_all x1, blocking collectives, on_device(): sums = lax.all_to_all(sums, PLANE, 0, 0, tiled=True)  16.8 us
    ppermute x1, starting transfers between devices, on_device(): right = lax.ppermute(first, SFC, backward)  14.1 us
    ppermute x1, waiting for transfers between devices, on_device(): left = lax.ppermute(last, SFC, forward)  2.59 us
    pallas_call x1, Pallas kernels, on_device(): in_vmem(own_part, (shape(2, 8, LANES, dtype=whole), shape(points, chunks,...  1.84 us
    pallas_call x1, Pallas kernels, on_device(): in_vmem(halo_part, (mid, mid, mid, shape(line, LANES)), 3 + len(prepared)...  1.57 us
  transfers between devices with their start and end apart: 2, of which 1 were waited for; matrix products, arithmetic and copies ran while one was open for 0% of the time, Pallas kernels for 2%

profile of v5, /device:TPU:1, one launch (start us, length us, event | category | flops | bytes accessed | tf_op | source)
XLA Modules:
  0.0 75.7 jit_solution(10224122520270792852)
XLA Ops:
  0.0 0.0 copy-start.5
  0.0 0.0 copy-start.1
  0.0 1.0 %copy-done.1 = f32[1,10,16,384]{3,2,1,0:T(8,128)S(1)} copy-done((f32[1,10,16,384]{3,2,1,0:T(8,128)S(1)}, f32[1,10,16,384]{3,2,1,0:T(8,128)}, u32[]{:S(2)}) %copy-start.1) | copy-done | bytes 245784
  1.0 0.0 copy-start.2
  1.0 0.0 copy-start.3
  1.0 0.0 copy-start.4
  1.0 0.0 copy-start
  1.0 14.1 %collective-permute-start = (f32[160,256]{1,0:T(8,128)S(1)}, f32[160,256]{1,0:T(8,128)S(1)}, u32[]{:S(2)}, u32[]{:S(2)}) collective-permute-start(f32[160,256]{1,0:T(8,128)S(1)} %get-tuple-element.18), channel_id=1, source_target_pairs={{16,0},{32,16},{48,32},{64,48},{80,64},{96,80},{112,96},{128,112},... | collective-permute-start | bytes 491528 | tf_op jit(solution)/shard_map/ppermute | solution.py:307
  15.1 0.0 collective-permute-start.1
  15.1 0.0 copy-done.5
  15.1 0.0 copy-done.2
  15.1 0.0 copy-done.3
  15.2 0.0 copy-done.4
  15.2 1.8 %shard_map.65 = (s32[2,8,128]{2,1,0:T(8,128)S(1)}, s32[16,3,80,128]{3,2,1,0:T(8,128)S(1)}, f32[2,8,128]{2,1,0:T(8,128)S(1)}, f32[4,3,16,128]{3,2,1,0:T(8,128)S(1...) custom-call(f32[160,384]{1,0:T(8,128)S(1)} %bitcast.21, ...), custom_call_target="tpu_custom_call" | custom-call | flops 1000000000 | tf_op jit(solution)/shard_map/pallas_call | solution.py:312
  17.0 0.0 collective-permute-done.right
  17.0 2.6 %collective-permute-done.1.left = f32[160,256]{1,0:T(8,128)S(1)} collective-permute-done((f32[160,256]{1,0:T(8,128)S(1)}, f32[160,256]{1,0:T(8,128)S(1)}, u32[]{:S(2)}, u32[]{:S(2)}) %collective-permute-start.1) | collective-permute-done | bytes 163872 | tf_op jit(solution)/shard_map/ppermute | solution.py:308
  19.6 0.0 copy-done
  19.6 1.6 %shard_map.66 = (f32[16,3,16,128]{3,2,1,0:T(8,128)S(1)}, f32[16,3,16,128]{3,2,1,0:T(8,128)S(1)}, f32[16,3,16,128]{3,2,1,0:T(8,128)S(1)}, f32[32,128]{1,0:T(8,128)S(1)}) custom-call(f32[160,256]{1,0:T(8,128)S(1)} %collective-permute-done.right, f32[160,256]{1,0:T(8,128)S(1)} %collective-permute-done.1.left, f32[16,384]{1,0:T(8,128)S(1)} %bitcast.18, ...), custom_call_target="tpu_custom_call" | custom-call | tf_op jit(solution)/shard_map/pallas_call | solution.py:330
  21.2 36.8 %all_to_all.22 = f32[32,1,128]{2,1,0:T(1,128)S(1)} all-to-all(f32[32,1,128]{2,1,0:T(1,128)S(1)} %bitcast.19), channel_id=1, replica_groups=mesh['sfc_0'=32,'sfc_1'=2,'lev_0'=4,'lev_1'=4] {'sfc_0'}, dimensions={0} | all-to-all | bytes 32768 | tf_op jit(solution)/shard_map/all_to_all | solution.py:340
  58.0 16.8 %all_to_all.23 = f32[32,1,128]{2,1,0:T(1,128)S(1)} all-to-all(f32[32,1,128]{2,1,0:T(1,128)S(1)} %bitcast.17), channel_id=1, replica_groups=mesh['sfc_0'=32,'sfc_1'=2,'lev_0'=4,'lev_1'=4] {'sfc_1','lev_0','lev_1'}, dimensions={0} | all-to-all | bytes 32768 | tf_op jit(solution)/shard_map/all_to_all | solution.py:342
  74.8 0.8 %shard_map.68 = f32[160,384]{1,0:T(8,128)} custom-call(f32[32,128]{1,0:T(8,128)S(1)} %bitcast.15, f32[16,3,16,128]{3,2,1,0:T(8,128)S(1)} %get-tuple-element.28.clip, f32[16,3,16,128]{3,2,1,0:T(8,128)S(1)} %get-tuple-element.29.up, f32[16,3,16,128]{3,2,1,0:T(8,128)S(1)} %get-tuple-element.30.down), custom_call_target="tpu_custom_call" | custom-call | tf_op jit(solution)/shard_map/pallas_call | solution.py:343
  (2 shorter events, 0.0 us)
Async XLA Ops:
  0.0 15.1 %copy-start.5 = (s32[1,2,128]{2,1,0:T(2,128)S(1)}, s32[1,2,128]{2,1,0:T(2,128)}, u32[]{:S(2)}) copy-start(s32[1,2,128]{2,1,0:T(2,128)} %param.11) | copy-start | bytes 3076
  0.0 1.0 %copy-start.1 = (f32[1,10,16,384]{3,2,1,0:T(8,128)S(1)}, f32[1,10,16,384]{3,2,1,0:T(8,128)}, u32[]{:S(2)}) copy-start(f32[1,10,16,384]{3,2,1,0:T(8,128)} %param.6) | copy-start | bytes 737284
  1.0 14.2 %copy-start.2 = (f32[2,1,16,384]{3,2,1,0:T(8,128)S(1)}, f32[2,1,16,384]{3,2,1,0:T(8,128)}, u32[]{:S(2)}) copy-start(f32[2,1,16,384]{3,2,1,0:T(8,128)} %param.9) | copy-start | bytes 147460
  1.0 14.2 %copy-start.3 = (f32[1,16,384]{2,1,0:T(8,128)S(1)}, f32[1,16,384]{2,1,0:T(8,128)}, u32[]{:S(2)}) copy-start(f32[1,16,384]{2,1,0:T(8,128)} %param.7) | copy-start | bytes 73732
  1.0 14.2 %copy-start.4 = (s32[1,16,384]{2,1,0:T(8,128)S(1)}, s32[1,16,384]{2,1,0:T(8,128)}, u32[]{:S(2)}) copy-start(s32[1,16,384]{2,1,0:T(8,128)} %param.10) | copy-start | bytes 73732
  1.0 18.6 %copy-start = (f32[1,16,384]{2,1,0:T(8,128)S(1)}, f32[1,16,384]{2,1,0:T(8,128)}, u32[]{:S(2)}) copy-start(f32[1,16,384]{2,1,0:T(8,128)} %param.8) | copy-start | bytes 73732
  1.0 16.0 %collective-permute-start = (f32[160,256]{1,0:T(8,128)S(1)}, f32[160,256]{1,0:T(8,128)S(1)}, u32[]{:S(2)}, u32[]{:S(2)}) collective-permute-start(f32[160,256]{1,0:T(8,128)S(1)} %get-tuple-element.18), channel_id=1, source_target_pairs={{16,0},{32,16},{48,32},{64,48},{80,64},{96,80},{112,96},{128,112},... | collective-permute-start | bytes 491528 | tf_op jit(solution)/shard_map/ppermute | solution.py:307
  15.1 4.5 %collective-permute-start.1 = (f32[160,256]{1,0:T(8,128)S(1)}, f32[160,256]{1,0:T(8,128)S(1)}, u32[]{:S(2)}, u32[]{:S(2)}) collective-permute-start(f32[160,256]{1,0:T(8,128)S(1)} %get-tuple-element.19), channel_id=1, source_target_pairs={{0,16},{16,32},{32,48},{48,64},{64,80},{80,96},{96,112},{112,128},... | collective-permute-start | bytes 491528 | tf_op jit(solution)/shard_map/ppermute | solution.py:308

commit v6 on v5

--- a/solution.py
+++ b/solution.py
@@ -329,7 +329,7 @@
     )(field, air_old[0], dep_coord[:, 0], dep_slot[0], fetch_list[0])
     clip, up, down, sums = in_vmem(
         halo_part,
-        (mid, mid, mid, shape(line, LANES)),
+        (mid, mid, mid, shape(plane, LANES)),
         3 + len(prepared),
         [
             pltpu.VMEM((4, tracers * points, LANES), real),
@@ -337,9 +337,9 @@
             pltpu.VMEM((chunks, points, LANES), real),
         ],
     )(right, left, air_new[0], *prepared)
+    sums = lax.all_to_all(sums, PLANE, 0, 0, tiled=True)
+    sums = in_vmem(relay, shape(line, LANES), 1)(sums)
     sums = lax.all_to_all(sums, LINE, 0, 0, tiled=True)
-    sums = in_vmem(relay, shape(plane, LANES), 1)(sums)
-    sums = lax.all_to_all(sums, PLANE, 0, 0, tiled=True)
     new = in_vmem(
         finish,
         shape(tracers * points, e_dev),

time: 75.9 us -> 74.4 us (0.980)
  blocking collectives: 53.6 us -> 52.2 us
    all_to_all x1, blocking collectives: 36.8 us -> 33.3 us  [on_device(): sums = lax.all_to_all(sums, LINE, 0, 0, tiled=True)]
    all_to_all x1, blocking collectives: 16.8 us -> 18.8 us  [on_device(): sums = lax.all_to_all(sums, PLANE, 0, 0, tiled=True)]
where the time goes in v6:
time: 74.4 us; the launch traced here: 74.2 us
  blocking collectives  52.2 us (70%)
  starting transfers between devices  14.1 us (19%)
  Pallas kernels  4.29 us (6%)
  waiting for transfers between devices  2.59 us (3%)
  local copies, waits for them, and re-layouts  0.98 us (1%)
    all_to_all x1, blocking collectives, on_device(): sums = lax.all_to_all(sums, LINE, 0, 0, tiled=True)  33.3 us
    all_to_all x1, blocking collectives, on_device(): sums = lax.all_to_all(sums, PLANE, 0, 0, tiled=True)  18.8 us
    ppermute x1, starting transfers between devices, on_device(): right = lax.ppermute(first, SFC, backward)  14.1 us
    ppermute x1, waiting for transfers between devices, on_device(): left = lax.ppermute(last, SFC, forward)  2.59 us
    pallas_call x1, Pallas kernels, on_device(): in_vmem(own_part, (shape(2, 8, LANES, dtype=whole), shape(points, chunks,...  1.84 us
    pallas_call x1, Pallas kernels, on_device(): in_vmem(halo_part, (mid, mid, mid, shape(plane, LANES)), 3 + len(prepared...  1.57 us
  transfers between devices with their start and end apart: 2, of which 1 were waited for; matrix products, arithmetic and copies ran while one was open for 0% of the time, Pallas kernels for 2%

profile of v6, /device:TPU:1, one launch (start us, length us, event | category | flops | bytes accessed | tf_op | source)
XLA Modules:
  0.0 74.2 jit_solution(3347469648313309560)
XLA Ops:
  0.0 0.0 copy-start.5
  0.0 0.0 copy-start.1
  0.0 1.0 %copy-done.1 = f32[1,10,16,384]{3,2,1,0:T(8,128)S(1)} copy-done((f32[1,10,16,384]{3,2,1,0:T(8,128)S(1)}, f32[1,10,16,384]{3,2,1,0:T(8,128)}, u32[]{:S(2)}) %copy-start.1) | copy-done | bytes 245784
  1.0 0.0 copy-start.2
  1.0 0.0 copy-start.3
  1.0 0.0 copy-start.4
  1.0 0.0 copy-start
  1.0 14.1 %collective-permute-start = (f32[160,256]{1,0:T(8,128)S(1)}, f32[160,256]{1,0:T(8,128)S(1)}, u32[]{:S(2)}, u32[]{:S(2)}) collective-permute-start(f32[160,256]{1,0:T(8,128)S(1)} %get-tuple-element.18), channel_id=1, source_target_pairs={{16,0},{32,16},{48,32},{64,48},{80,64},{96,80},{112,96},{128,112},... | collective-permute-start | bytes 491528 | tf_op jit(solution)/shard_map/ppermute | solution.py:307
  15.1 0.0 collective-permute-start.1
  15.1 0.0 copy-done.5
  15.1 0.0 copy-done.2
  15.1 0.0 copy-done.3
  15.2 0.0 copy-done.4
  15.2 1.8 %shard_map.65 = (s32[2,8,128]{2,1,0:T(8,128)S(1)}, s32[16,3,80,128]{3,2,1,0:T(8,128)S(1)}, f32[2,8,128]{2,1,0:T(8,128)S(1)}, f32[4,3,16,128]{3,2,1,0:T(8,128)S(1...) custom-call(f32[160,384]{1,0:T(8,128)S(1)} %bitcast.21, ...), custom_call_target="tpu_custom_call" | custom-call | flops 1000000000 | tf_op jit(solution)/shard_map/pallas_call | solution.py:312
  17.0 0.0 collective-permute-done.right
  17.0 2.6 %collective-permute-done.1.left = f32[160,256]{1,0:T(8,128)S(1)} collective-permute-done((f32[160,256]{1,0:T(8,128)S(1)}, f32[160,256]{1,0:T(8,128)S(1)}, u32[]{:S(2)}, u32[]{:S(2)}) %collective-permute-start.1) | collective-permute-done | bytes 163872 | tf_op jit(solution)/shard_map/ppermute | solution.py:308
  19.6 0.0 copy-done
  19.6 1.6 %shard_map.66 = (f32[16,3,16,128]{3,2,1,0:T(8,128)S(1)}, f32[16,3,16,128]{3,2,1,0:T(8,128)S(1)}, f32[16,3,16,128]{3,2,1,0:T(8,128)S(1)}, f32[32,128]{1,0:T(8,128)S(1)}) custom-call(f32[160,256]{1,0:T(8,128)S(1)} %collective-permute-done.right, f32[160,256]{1,0:T(8,128)S(1)} %collective-permute-done.1.left, f32[16,384]{1,0:T(8,128)S(1)} %bitcast.18, ...), custom_call_target="tpu_custom_call" | custom-call | tf_op jit(solution)/shard_map/pallas_call | solution.py:330
  21.2 18.8 %all_to_all.22 = f32[32,1,128]{2,1,0:T(1,128)S(1)} all-to-all(f32[32,1,128]{2,1,0:T(1,128)S(1)} %bitcast.19), channel_id=1, replica_groups=mesh['sfc_0'=32,'sfc_1'=2,'lev_0'=4,'lev_1'=4] {'sfc_1','lev_0','lev_1'}, dimensions={0} | all-to-all | bytes 32768 | tf_op jit(solution)/shard_map/all_to_all | solution.py:340
  40.0 33.3 %all_to_all.23 = f32[32,1,128]{2,1,0:T(1,128)S(1)} all-to-all(f32[32,1,128]{2,1,0:T(1,128)S(1)} %bitcast.17), channel_id=1, replica_groups=mesh['sfc_0'=32,'sfc_1'=2,'lev_0'=4,'lev_1'=4] {'sfc_0'}, dimensions={0} | all-to-all | bytes 32768 | tf_op jit(solution)/shard_map/all_to_all | solution.py:342
  73.4 0.8 %shard_map.68 = f32[160,384]{1,0:T(8,128)} custom-call(f32[32,128]{1,0:T(8,128)S(1)} %bitcast.15, f32[16,3,16,128]{3,2,1,0:T(8,128)S(1)} %get-tuple-element.28.clip, f32[16,3,16,128]{3,2,1,0:T(8,128)S(1)} %get-tuple-element.29.up, f32[16,3,16,128]{3,2,1,0:T(8,128)S(1)} %get-tuple-element.30.down), custom_call_target="tpu_custom_call" | custom-call | tf_op jit(solution)/shard_map/pallas_call | solution.py:343
  (2 shorter events, 0.0 us)
Async XLA Ops:
  0.0 15.1 %copy-start.5 = (s32[1,2,128]{2,1,0:T(2,128)S(1)}, s32[1,2,128]{2,1,0:T(2,128)}, u32[]{:S(2)}) copy-start(s32[1,2,128]{2,1,0:T(2,128)} %param.11) | copy-start | bytes 3076
  0.0 1.0 %copy-start.1 = (f32[1,10,16,384]{3,2,1,0:T(8,128)S(1)}, f32[1,10,16,384]{3,2,1,0:T(8,128)}, u32[]{:S(2)}) copy-start(f32[1,10,16,384]{3,2,1,0:T(8,128)} %param.6) | copy-start | bytes 737284
  1.0 14.2 %copy-start.2 = (f32[2,1,16,384]{3,2,1,0:T(8,128)S(1)}, f32[2,1,16,384]{3,2,1,0:T(8,128)}, u32[]{:S(2)}) copy-start(f32[2,1,16,384]{3,2,1,0:T(8,128)} %param.9) | copy-start | bytes 147460
  1.0 14.2 %copy-start.3 = (f32[1,16,384]{2,1,0:T(8,128)S(1)}, f32[1,16,384]{2,1,0:T(8,128)}, u32[]{:S(2)}) copy-start(f32[1,16,384]{2,1,0:T(8,128)} %param.7) | copy-start | bytes 73732
  1.0 14.2 %copy-start.4 = (s32[1,16,384]{2,1,0:T(8,128)S(1)}, s32[1,16,384]{2,1,0:T(8,128)}, u32[]{:S(2)}) copy-start(s32[1,16,384]{2,1,0:T(8,128)} %param.10) | copy-start | bytes 73732
  1.0 18.6 %copy-start = (f32[1,16,384]{2,1,0:T(8,128)S(1)}, f32[1,16,384]{2,1,0:T(8,128)}, u32[]{:S(2)}) copy-start(f32[1,16,384]{2,1,0:T(8,128)} %param.8) | copy-start | bytes 73732
  1.0 16.0 %collective-permute-start = (f32[160,256]{1,0:T(8,128)S(1)}, f32[160,256]{1,0:T(8,128)S(1)}, u32[]{:S(2)}, u32[]{:S(2)}) collective-permute-start(f32[160,256]{1,0:T(8,128)S(1)} %get-tuple-element.18), channel_id=1, source_target_pairs={{16,0},{32,16},{48,32},{64,48},{80,64},{96,80},{112,96},{128,112},... | collective-permute-start | bytes 491528 | tf_op jit(solution)/shard_map/ppermute | solution.py:307
  15.1 4.5 %collective-permute-start.1 = (f32[160,256]{1,0:T(8,128)S(1)}, f32[160,256]{1,0:T(8,128)S(1)}, u32[]{:S(2)}, u32[]{:S(2)}) collective-permute-start(f32[160,256]{1,0:T(8,128)S(1)} %get-tuple-element.19), channel_id=1, source_target_pairs={{0,16},{16,32},{32,48},{48,64},{64,80},{80,96},{96,112},{112,128},... | collective-permute-start | bytes 491528 | tf_op jit(solution)/shard_map/ppermute | solution.py:308

commit v7 on v6

--- a/solution.py
+++ b/solution.py
@@ -13,11 +13,12 @@
 PLANE = ("sfc_1", "lev_0", "lev_1")
 LINE = "sfc_0"
 NODES = (-1.0, -0.4472135954999579, 0.4472135954999579, 1.0)
+REGISTERS = 20
 UNROLL = 16
 OWN_UNROLL = 16
-STEPS = 32767.0
 GRANT = 12 * 1024 * 1024
 WORK = 1_000_000_000
+LOAD = 10_000_000_000
 
 
 def basis(coord):
@@ -72,37 +73,24 @@
     return old, jnp.where(sub == 0, tails[0], jnp.where(sub == 4, tails[1], zero))
 
 
-def fixed(x):
-    return (x * STEPS + 0.5).astype(jnp.int32)
-
-
-def pair(wide, c, k):
-    return fixed(wide[c, rows(2 * k), :]) | (fixed(wide[c, rows(2 * k + 1), :]) << 16)
-
-
-def halves(x):
-    first = (x & 0xFFFF).astype(jnp.float32)
-    return first, lax.shift_right_logical(x, 16).astype(jnp.float32)
-
-
-def gather(pairs, along_a, along_b, stack):
+def gather(value, along_a, along_b, stack):
     def inner(first):
         total = low = high = None
-        for k in range(2):
-            for q, x in enumerate(halves(pairs(first + k))):
-                low = x if low is None else jnp.minimum(low, x)
-                high = x if high is None else jnp.maximum(high, x)
-                term = along_b[2 * k + q] * x
-                total = term if total is None else total + term
+        for q in range(4):
+            x = value(first + q)
+            low = x if low is None else jnp.minimum(low, x)
+            high = x if high is None else jnp.maximum(high, x)
+            term = along_b[q] * x
+            total = term if total is None else total + term
         return total, low, high
 
     interp, low, high = inner(0)
     interp = interp * along_a[0]
     for i in range(1, 4):
-        more, least, most = inner(2 * i)
+        more, least, most = inner(4 * i)
         interp = interp + along_a[i] * more
         low, high = jnp.minimum(low, least), jnp.maximum(high, most)
-    tail, tail_low, tail_high = inner(8)
+    tail, tail_low, tail_high = inner(16)
     tail = group_of_four(tail * stack, jnp.add)
     tail_low = group_of_four(tail_low, jnp.minimum)
     tail_high = group_of_four(tail_high, jnp.maximum)
@@ -127,8 +115,8 @@
         wide[c] = field[:, c * LANES : (c + 1) * LANES]
         slots[c] = slot[:, c * LANES : (c + 1) * LANES]
     for c in range(chunks):
-        for k in range(10):
-            table[c, 8 * k : 8 * k + 8, :] = pair(wide, c, k)
+        for v in range(REGISTERS):
+            table[c, 8 * v : 8 * v + 8, :] = wide[c, rows(v), :]
 
     def step(k, carry):
         for u in range(OWN_UNROLL):
@@ -137,8 +125,8 @@
                 where = broadcast_row(slots, n, e)
                 near, chunk = where & (LANES - 1), where >> 7
                 masks = [chunk == c for c in range(1, chunks)]
-                for k2 in range(10):
-                    at = slice(8 * k2, 8 * k2 + 8)
+                for v in range(REGISTERS):
+                    at = slice(8 * v, 8 * v + 8)
                     x = pick(table[0, at, :], near)
                     for c, mask in enumerate(masks):
                         x = jnp.where(mask, pick(table[c + 1, at, :], near), x)
@@ -158,48 +146,66 @@
             stacked[c, pl.ds(i + 4, points, stride=8), :] = terms_a[i][:, cols]
 
 
-def halo_part(
-    right, left, air_new, picks, own, old, along_a, along_b, stacked, slots,
+def band_table(band, idx, wide, table):
+    for c in range(2):
+        wide[c] = band[:, c * LANES : (c + 1) * LANES]
+    near, far = idx & (LANES - 1), idx >= LANES
+    for v in range(REGISTERS):
+        first = pick(wide[0, rows(v), :], near)
+        second = pick(wide[1, rows(v), :], near)
+        table[8 * v : 8 * v + 8, :] = jnp.where(far, second, first)
+
+
+def right_part(right, picks, own, slots, merged_out, wide, table):
+    points, chunks = own.shape[:2]
+    band_table(right, picks[1], wide, table)
+
+    def step(k, carry):
+        for u in range(UNROLL):
+            n = k * UNROLL + u
+            for e in range(chunks):
+                where = broadcast_row(slots, n, e)
+                near, at_right = where & (LANES - 1), (where >> 7) == chunks + 1
+                for v in range(REGISTERS):
+                    at = slice(8 * v, 8 * v + 8)
+                    x = pick(table[at, :], near)
+                    merged_out[n, e, at, :] = jnp.where(at_right, x, own[n, e, at, :])
+        return carry
+
+    lax.fori_loop(0, points // UNROLL, step, 0)
+
+
+def left_part(
+    left, air_new, picks, merged, old, along_a, along_b, stacked, slots,
     clip_out, up_out, down_out, sums_out,
     wide, table, airs,
 ):
-    points, chunks = own.shape[:2]
-    count = chunks * LANES
+    points, chunks = merged.shape[:2]
     sub = lax.broadcasted_iota(jnp.int32, (8, LANES), 0)
     lane = lax.broadcasted_iota(jnp.int32, (8, LANES), 1)
     zero = jnp.zeros((8, LANES), jnp.float32)
     for c in range(chunks):
         airs[c] = air_new[:, c * LANES : (c + 1) * LANES]
-    for side, band in enumerate((left, right)):
-        for c in range(2):
-            wide[2 * side + c] = band[:, c * LANES : (c + 1) * LANES]
-    for side in range(2):
-        idx = picks[side]
-        near, far = idx & (LANES - 1), idx >= LANES
-        for k in range(10):
-            first = pick(pair(wide, 2 * side, k), near)
-            second = pick(pair(wide, 2 * side + 1, k), near)
-            table[side, 8 * k : 8 * k + 8, :] = jnp.where(far, second, first)
+    band_table(left, picks[0], wide, table)
 
     def group(n, e, acc):
         where = broadcast_row(slots, n, e)
-        near, at_right, halo = where & (LANES - 1), where >= count + LANES, where >= count
-
-        def pairs(k):
-            at = slice(8 * k, 8 * k + 8)
-            x = jnp.where(at_right, pick(table[1, at, :], near), pick(table[0, at, :], near))
-            return jnp.where(halo, x, own[n, e, at, :])
+        near, at_left = where & (LANES - 1), (where >> 7) == chunks
+
+        def value(v):
+            at = slice(8 * v, 8 * v + 8)
+            return jnp.where(at_left, pick(table[at, :], near), merged[n, e, at, :])
 
         row_a, row_b = (
             [broadcast_row(ref, n, i, e) for i in range(4)] for ref in (along_a, along_b)
         )
-        parts = gather(pairs, row_a, row_b, stacked[e, pl.ds(pl.multiple_of(8 * n, 8), 8), :])
+        parts = gather(value, row_a, row_b, stacked[e, pl.ds(pl.multiple_of(8 * n, 8), 8), :])
         air = broadcast_row(airs, n, e)
         acc = list(acc)
         for h, (f, lo, hi) in enumerate(parts):
             at = (n, e, slice(8 * h, 8 * h + 8), slice(None))
             f = jnp.minimum(jnp.maximum(f, lo), hi)
-            f, up, down = f * (1.0 / STEPS), (hi - f) * (1.0 / STEPS), (f - lo) * (1.0 / STEPS)
+            up, down = hi - f, f - lo
             clip_out[at], up_out[at], down_out[at] = f, up, down
             acc[3 * h] = acc[3 * h] - air * f
             acc[3 * h + 1] = acc[3 * h + 1] + air * up
@@ -300,7 +306,7 @@
         return jax.ShapeDtypeStruct(dims, dtype)
 
     band = shape(tracers * points, BAND)
-    last, first = in_vmem(bands, (band, band), 1, work=WORK)(field)
+    last, first = in_vmem(bands, (band, band), 1, work=LOAD)(field)
     count = lax.axis_size(SFC)
     forward = [(i, (i + 1) % count) for i in range(count)]
     backward = [(target, source) for source, target in forward]
@@ -309,11 +315,14 @@
     mid = shape(points, chunks, 16, LANES)
     plane, line = lax.axis_size(PLANE), lax.axis_size(LINE)
     terms = shape(4, chunks, points, LANES)
-    prepared = in_vmem(
+    table = pltpu.VMEM((8 * REGISTERS, LANES), real)
+    wide = pltpu.VMEM((2, tracers * points, LANES), real)
+    picked = shape(points, chunks, 8 * REGISTERS, LANES)
+    picks, own, *rest = in_vmem(
         own_part,
         (
             shape(2, 8, LANES, dtype=whole),
-            shape(points, chunks, 80, LANES, dtype=whole),
+            picked,
             shape(2, 8, LANES),
             terms,
             terms,
@@ -323,20 +332,17 @@
         5,
         [
             pltpu.VMEM((chunks, tracers * points, LANES), real),
-            pltpu.VMEM((chunks, 80, LANES), whole),
+            pltpu.VMEM((chunks, 8 * REGISTERS, LANES), real),
         ],
         WORK,
     )(field, air_old[0], dep_coord[:, 0], dep_slot[0], fetch_list[0])
+    merged = in_vmem(right_part, picked, 4, [wide, table], WORK)(right, picks, own, rest[-1])
     clip, up, down, sums = in_vmem(
-        halo_part,
+        left_part,
         (mid, mid, mid, shape(plane, LANES)),
-        3 + len(prepared),
-        [
-            pltpu.VMEM((4, tracers * points, LANES), real),
-            pltpu.VMEM((2, 80, LANES), whole),
-            pltpu.VMEM((chunks, points, LANES), real),
-        ],
-    )(right, left, air_new[0], *prepared)
+        4 + len(rest),
+        [wide, table, pltpu.VMEM((chunks, points, LANES), real)],
+    )(left, air_new[0], picks, merged, *rest)
     sums = lax.all_to_all(sums, PLANE, 0, 0, tiled=True)
     sums = in_vmem(relay, shape(line, LANES), 1)(sums)
     sums = lax.all_to_all(sums, LINE, 0, 0, tiled=True)

time: 74.4 us -> 74.4 us (level)
  Pallas kernels: 4.29 us -> 7.09 us
  waiting for transfers between devices: 2.59 us -> 0.01 us
    pallas_call x3 -> x4, Pallas kernels: 3.43 us -> 6.23 us  [the longest x1 3.33 us: on_device(): in_vmem(own_part, (shape(2, 8, LANES, dtype=whole), picked, shape(2, 8, L...]
    ppermute x1, waiting for transfers between devices: 2.59 us -> 0.01 us  [on_device(): left = lax.ppermute(last, SFC, forward)]
  transfers between devices with their start and end apart: 2 -> 2, of which waited for: 1 -> 0; matrix products, arithmetic and copies ran while one was open for 0% -> 0% of each run, Pallas kernels for 2% -> 6%
where the time goes in v7:
time: 74.4 us; the launch traced here: 74.1 us
  blocking collectives  51.9 us (70%)
  starting transfers between devices  14.1 us (19%)
  Pallas kernels  7.09 us (10%)
  local copies, waits for them, and re-layouts  0.96 us (1%)
    all_to_all x1, blocking collectives, on_device(): sums = lax.all_to_all(sums, LINE, 0, 0, tiled=True)  33.3 us
    all_to_all x1, blocking collectives, on_device(): sums = lax.all_to_all(sums, PLANE, 0, 0, tiled=True)  18.5 us
    ppermute x1, starting transfers between devices, on_device(): right = lax.ppermute(first, SFC, backward)  14.1 us
    pallas_call x1, Pallas kernels, on_device(): in_vmem(own_part, (shape(2, 8, LANES, dtype=whole), picked, shape(2, 8, L...  3.33 us
    pallas_call x1, Pallas kernels, on_device(): in_vmem(left_part, (mid, mid, mid, shape(plane, LANES)), 4 + len(rest), [...  1.52 us
  transfers between devices with their start and end apart: 2, of which 0 were waited for; matrix products, arithmetic and copies ran while one was open for 0% of the time, Pallas kernels for 6%

profile of v7, /device:TPU:1, one launch (start us, length us, event | category | flops | bytes accessed | tf_op | source)
XLA Modules:
  0.0 74.1 jit_solution(476098000274657377)
XLA Ops:
  0.0 0.0 copy-start.1
  0.0 0.9 %copy-done.1 = f32[1,10,16,384]{3,2,1,0:T(8,128)S(1)} copy-done((f32[1,10,16,384]{3,2,1,0:T(8,128)S(1)}, f32[1,10,16,384]{3,2,1,0:T(8,128)}, u32[]{:S(2)}) %copy-start.1) | copy-done | bytes 245784
  0.9 0.0 copy-start.2
  0.9 0.0 copy-start.3
  0.9 0.0 copy-start.4
  1.0 0.0 copy-start.5
  1.0 14.1 %collective-permute-start.1 = (f32[160,256]{1,0:T(8,128)S(1)}, f32[160,256]{1,0:T(8,128)S(1)}, u32[]{:S(2)}, u32[]{:S(2)}) collective-permute-start(f32[160,256]{1,0:T(8,128)S(1)} %get-tuple-element.20), channel_id=1, source_target_pairs={{16,0},{32,16},{48,32},{64,48},{80,64},{96,80},{112,96},{128,112},... | collective-permute-start | bytes 491528 | tf_op jit(solution)/shard_map/ppermute | solution.py:313
  15.1 0.0 collective-permute-start
  15.1 0.0 copy-done.2
  15.1 0.0 copy-done.3
  15.1 0.0 copy-done.4
  15.1 0.0 copy-done.5
  15.1 3.3 %shard_map.65 = (s32[2,8,128]{2,1,0:T(8,128)S(1)}, f32[16,3,160,128]{3,2,1,0:T(8,128)S(1)}, f32[2,8,128]{2,1,0:T(8,128)S(1)}, f32[4,3,16,128]{3,2,1,0:T(8,128)S(...) custom-call(f32[160,384]{1,0:T(8,128)S(1)} %bitcast.21, ...), custom_call_target="tpu_custom_call" | custom-call | flops 1000000000 | tf_op jit(solution)/shard_map/pallas_call | solution.py:321
  18.5 0.0 collective-permute-done.1.right
  18.5 0.0 copy-start
  18.5 1.4 %shard_map.66.merged = f32[16,3,160,128]{3,2,1,0:T(8,128)S(1)} custom-call(f32[160,256]{1,0:T(8,128)S(1)} %collective-permute-done.1.right, s32[2,8,128]{2,1,0:T(8,128)S(1)} %get-tuple-element.19.picks, f32[16,3,160,128]{3,2,1,0:T(8,128)S(1)} %get-tuple-element.21.own, s32[3,16,128]{2,1,0:T(8,128)S(1)} %get-tuple-element.22.slots), custom_call_target="tpu_custom_call" | custom-call | flops 1000000000 | tf_op jit(solution)/shard_map/pallas_call | solution.py:339
  19.9 0.0 collective-permute-done.left
  19.9 0.0 copy-done
  19.9 1.5 %shard_map.67 = (f32[16,3,16,128]{3,2,1,0:T(8,128)S(1)}, f32[16,3,16,128]{3,2,1,0:T(8,128)S(1)}, f32[16,3,16,128]{3,2,1,0:T(8,128)S(1)}, f32[32,128]{1,0:T(8,128)S(1)}) custom-call(f32[160,256]{1,0:T(8,128)S(1)} %collective-permute-done.left, f32[16,384]{1,0:T(8,128)S(1)} %bitcast.18, s32[2,8,128]{2,1,0:T(8,128)S(1)} %get-tuple-element.19.picks, ...), custom_call_target="tpu_custom_call" | custom-call | tf_op jit(solution)/shard_map/pallas_call | solution.py:340
  21.4 18.5 %all_to_all.22 = f32[32,1,128]{2,1,0:T(1,128)S(1)} all-to-all(f32[32,1,128]{2,1,0:T(1,128)S(1)} %bitcast.19), channel_id=1, replica_groups=mesh['sfc_0'=32,'sfc_1'=2,'lev_0'=4,'lev_1'=4] {'sfc_1','lev_0','lev_1'}, dimensions={0} | all-to-all | bytes 32768 | tf_op jit(solution)/shard_map/all_to_all | solution.py:346
  40.0 33.3 %all_to_all.23 = f32[32,1,128]{2,1,0:T(1,128)S(1)} all-to-all(f32[32,1,128]{2,1,0:T(1,128)S(1)} %bitcast.17), channel_id=1, replica_groups=mesh['sfc_0'=32,'sfc_1'=2,'lev_0'=4,'lev_1'=4] {'sfc_0'}, dimensions={0} | all-to-all | bytes 32768 | tf_op jit(solution)/shard_map/all_to_all | solution.py:348
  73.3 0.8 %shard_map.69 = f32[160,384]{1,0:T(8,128)} custom-call(f32[32,128]{1,0:T(8,128)S(1)} %bitcast.15, f32[16,3,16,128]{3,2,1,0:T(8,128)S(1)} %get-tuple-element.28.clip, f32[16,3,16,128]{3,2,1,0:T(8,128)S(1)} %get-tuple-element.29.up, f32[16,3,16,128]{3,2,1,0:T(8,128)S(1)} %get-tuple-element.30.down), custom_call_target="tpu_custom_call" | custom-call | tf_op jit(solution)/shard_map/pallas_call | solution.py:349
  (2 shorter events, 0.0 us)
Async XLA Ops:
  0.0 0.9 %copy-start.1 = (f32[1,10,16,384]{3,2,1,0:T(8,128)S(1)}, f32[1,10,16,384]{3,2,1,0:T(8,128)}, u32[]{:S(2)}) copy-start(f32[1,10,16,384]{3,2,1,0:T(8,128)} %param.6) | copy-start | bytes 737284
  0.9 14.2 %copy-start.2 = (f32[2,1,16,384]{3,2,1,0:T(8,128)S(1)}, f32[2,1,16,384]{3,2,1,0:T(8,128)}, u32[]{:S(2)}) copy-start(f32[2,1,16,384]{3,2,1,0:T(8,128)} %param.9) | copy-start | bytes 147460
  0.9 14.2 %copy-start.3 = (f32[1,16,384]{2,1,0:T(8,128)S(1)}, f32[1,16,384]{2,1,0:T(8,128)}, u32[]{:S(2)}) copy-start(f32[1,16,384]{2,1,0:T(8,128)} %param.7) | copy-start | bytes 73732
  0.9 14.2 %copy-start.4 = (s32[1,16,384]{2,1,0:T(8,128)S(1)}, s32[1,16,384]{2,1,0:T(8,128)}, u32[]{:S(2)}) copy-start(s32[1,16,384]{2,1,0:T(8,128)} %param.10) | copy-start | bytes 73732
  1.0 14.2 %copy-start.5 = (s32[1,2,128]{2,1,0:T(2,128)S(1)}, s32[1,2,128]{2,1,0:T(2,128)}, u32[]{:S(2)}) copy-start(s32[1,2,128]{2,1,0:T(2,128)} %param.11) | copy-start | bytes 3076
  1.0 17.5 %collective-permute-start.1 = (f32[160,256]{1,0:T(8,128)S(1)}, f32[160,256]{1,0:T(8,128)S(1)}, u32[]{:S(2)}, u32[]{:S(2)}) collective-permute-start(f32[160,256]{1,0:T(8,128)S(1)} %get-tuple-element.20), channel_id=1, source_target_pairs={{16,0},{32,16},{48,32},{64,48},{80,64},{96,80},{112,96},{128,112},... | collective-permute-start | bytes 491528 | tf_op jit(solution)/shard_map/ppermute | solution.py:313
  15.1 4.8 %collective-permute-start = (f32[160,256]{1,0:T(8,128)S(1)}, f32[160,256]{1,0:T(8,128)S(1)}, u32[]{:S(2)}, u32[]{:S(2)}) collective-permute-start(f32[160,256]{1,0:T(8,128)S(1)} %get-tuple-element.18), channel_id=1, source_target_pairs={{0,16},{16,32},{32,48},{48,64},{64,80},{80,96},{96,112},{112,128},... | collective-permute-start | bytes 491528 | tf_op jit(solution)/shard_map/ppermute | solution.py:314
  18.5 1.4 %copy-start = (f32[1,16,384]{2,1,0:T(8,128)S(1)}, f32[1,16,384]{2,1,0:T(8,128)}, u32[]{:S(2)}) copy-start(f32[1,16,384]{2,1,0:T(8,128)} %param.8) | copy-start | bytes 73732

commit v8 on v7

--- a/solution.py
+++ b/solution.py
@@ -14,7 +14,6 @@
 LINE = "sfc_0"
 NODES = (-1.0, -0.4472135954999579, 0.4472135954999579, 1.0)
 REGISTERS = 20
-UNROLL = 16
 OWN_UNROLL = 16
 GRANT = 12 * 1024 * 1024
 WORK = 1_000_000_000
@@ -158,11 +157,11 @@
 
 def right_part(right, picks, own, slots, merged_out, wide, table):
     points, chunks = own.shape[:2]
-    band_table(right, picks[1], wide, table)
-
-    def step(k, carry):
-        for u in range(UNROLL):
-            n = k * UNROLL + u
+
+    @pl.when(lax.axis_index("sfc_1") == 0)
+    def _():
+        band_table(right, picks[1], wide, table)
+        for n in range(points):
             for e in range(chunks):
                 where = broadcast_row(slots, n, e)
                 near, at_right = where & (LANES - 1), (where >> 7) == chunks + 1
@@ -170,13 +169,10 @@
                     at = slice(8 * v, 8 * v + 8)
                     x = pick(table[at, :], near)
                     merged_out[n, e, at, :] = jnp.where(at_right, x, own[n, e, at, :])
-        return carry
-
-    lax.fori_loop(0, points // UNROLL, step, 0)
-
-
-def left_part(
-    left, air_new, picks, merged, old, along_a, along_b, stacked, slots,
+
+
+def last_part(
+    left, right, air_new, picks, merged, old, along_a, along_b, stacked, slots,
     clip_out, up_out, down_out, sums_out,
     wide, table, airs,
 ):
@@ -186,20 +182,23 @@
     zero = jnp.zeros((8, LANES), jnp.float32)
     for c in range(chunks):
         airs[c] = air_new[:, c * LANES : (c + 1) * LANES]
-    band_table(left, picks[0], wide, table)
-
-    def group(n, e, acc):
+
+    def group(n, e, acc, sides):
         where = broadcast_row(slots, n, e)
-        near, at_left = where & (LANES - 1), (where >> 7) == chunks
+        near, chunk = where & (LANES - 1), where >> 7
+        masks = [(side, chunk == chunks + side) for side in sides]
 
         def value(v):
             at = slice(8 * v, 8 * v + 8)
-            return jnp.where(at_left, pick(table[at, :], near), merged[n, e, at, :])
+            x = merged[n, e, at, :]
+            for side, mask in masks:
+                x = jnp.where(mask, pick(table[side, at, :], near), x)
+            return x
 
         row_a, row_b = (
             [broadcast_row(ref, n, i, e) for i in range(4)] for ref in (along_a, along_b)
         )
-        parts = gather(value, row_a, row_b, stacked[e, pl.ds(pl.multiple_of(8 * n, 8), 8), :])
+        parts = gather(value, row_a, row_b, stacked[e, 8 * n : 8 * n + 8, :])
         air = broadcast_row(airs, n, e)
         acc = list(acc)
         for h, (f, lo, hi) in enumerate(parts):
@@ -212,23 +211,33 @@
             acc[3 * h + 2] = acc[3 * h + 2] + air * down
         return tuple(acc)
 
-    def step(k, acc):
-        for u in range(UNROLL):
+    def run(sides):
+        for side in sides:
+            band_table((left, right)[side], picks[side], wide.at[side], table.at[side])
+        acc = (old[0], zero, zero, old[1], zero, zero)
+        for n in range(points):
             for e in range(chunks):
-                acc = group(k * UNROLL + u, e, acc)
-        return acc
-
-    acc = lax.fori_loop(0, points // UNROLL, step, (old[0], zero, zero, old[1], zero, zero))
-    row_of = zero
-    for k in range(6):
-        total = jnp.broadcast_to(jnp.sum(acc[k], axis=1, keepdims=True), (8, LANES))
-        keep = lane == 8 * k + sub
-        if k >= 3:
-            keep = keep & ((sub & 3) == 0)
-        row_of = row_of + jnp.where(keep, total, zero)
-    row_of = all_sublanes(row_of)
-    for k in range(sums_out.shape[0] // 8):
-        sums_out[8 * k : 8 * k + 8, :] = row_of
+                acc = group(n, e, acc, sides)
+        row_of = zero
+        for k in range(6):
+            total = jnp.broadcast_to(jnp.sum(acc[k], axis=1, keepdims=True), (8, LANES))
+            keep = lane == 8 * k + sub
+            if k >= 3:
+                keep = keep & ((sub & 3) == 0)
+            row_of = row_of + jnp.where(keep, total, zero)
+        row_of = all_sublanes(row_of)
+        for k in range(sums_out.shape[0] // 8):
+            sums_out[8 * k : 8 * k + 8, :] = row_of
+
+    core = lax.axis_index("sfc_1")
+
+    @pl.when(core == 0)
+    def _():
+        run((0,))
+
+    @pl.when(core != 0)
+    def _():
+        run((0, 1))
 
 
 def add_rows(parts):
@@ -278,7 +287,7 @@
         copy.wait()
 
 
-def in_vmem(kernel, out_shape, count, scratch=(), work=0, out_space=pltpu.VMEM):
+def in_vmem(kernel, out_shape, count, scratch=(), work=0, out_space=pltpu.VMEM, in_place=()):
     spec = pl.BlockSpec(memory_space=pltpu.VMEM)
     return pl.pallas_call(
         kernel,
@@ -286,6 +295,7 @@
         in_specs=[spec] * count,
         out_specs=jax.tree.map(lambda _: pl.BlockSpec(memory_space=out_space), out_shape),
         scratch_shapes=scratch,
+        input_output_aliases=dict(in_place),
         cost_estimate=pl.CostEstimate(flops=work, bytes_accessed=0, transcendentals=0),
         compiler_params=pltpu.CompilerParams(vmem_limit_bytes=GRANT),
     )
@@ -336,13 +346,19 @@
         ],
         WORK,
     )(field, air_old[0], dep_coord[:, 0], dep_slot[0], fetch_list[0])
-    merged = in_vmem(right_part, picked, 4, [wide, table], WORK)(right, picks, own, rest[-1])
+    merged = in_vmem(right_part, picked, 4, [wide, table], WORK, in_place=((2, 0),))(
+        right, picks, own, rest[-1]
+    )
     clip, up, down, sums = in_vmem(
-        left_part,
+        last_part,
         (mid, mid, mid, shape(plane, LANES)),
-        4 + len(rest),
-        [wide, table, pltpu.VMEM((chunks, points, LANES), real)],
-    )(left, air_new[0], picks, merged, *rest)
+        5 + len(rest),
+        [
+            pltpu.VMEM((2, 2, tracers * points, LANES), real),
+            pltpu.VMEM((2, 8 * REGISTERS, LANES), real),
+            pltpu.VMEM((chunks, points, LANES), real),
+        ],
+    )(left, right, air_new[0], picks, merged, *rest)
     sums = lax.all_to_all(sums, PLANE, 0, 0, tiled=True)
     sums = in_vmem(relay, shape(line, LANES), 1)(sums)
     sums = lax.all_to_all(sums, LINE, 0, 0, tiled=True)

time: 74.4 us -> 74.6 us (level)
  waiting for transfers between devices: 0.01 us -> 1.07 us
    ppermute x1, waiting for transfers between devices: 0.01 us -> 1.06 us  [on_device(): left = lax.ppermute(last, SFC, forward)]
  transfers between devices with their start and end apart: 2 -> 2, of which waited for: 0 -> 1; matrix products, arithmetic and copies ran while one was open for 0% -> 0% of each run, Pallas kernels for 6% -> 4%
where the time goes in v8:
time: 74.6 us; the launch traced here: 74.4 us
  blocking collectives  51.5 us (69%)
  starting transfers between devices  14.1 us (19%)
  Pallas kernels  6.71 us (9%)
  waiting for transfers between devices  1.07 us (1%)
  local copies, waits for them, and re-layouts  0.96 us (1%)
    all_to_all x1, blocking collectives, on_device(): sums = lax.all_to_all(sums, LINE, 0, 0, tiled=True)  33.6 us
    all_to_all x1, blocking collectives, on_device(): sums = lax.all_to_all(sums, PLANE, 0, 0, tiled=True)  17.9 us
    ppermute x1, starting transfers between devices, on_device(): right = lax.ppermute(first, SFC, backward)  14.1 us
    pallas_call x1, Pallas kernels, on_device(): in_vmem(own_part, (shape(2, 8, LANES, dtype=whole), picked, shape(2, 8, L...  3.33 us
    pallas_call x1, Pallas kernels, on_device(): in_vmem(last_part, (mid, mid, mid, shape(plane, LANES)), 5 + len(rest), [...  2.48 us
  transfers between devices with their start and end apart: 2, of which 1 were waited for; matrix products, arithmetic and copies ran while one was open for 0% of the time, Pallas kernels for 4%

profile of v8, /device:TPU:1, one launch (start us, length us, event | category | flops | bytes accessed | tf_op | source)
XLA Modules:
  0.0 74.4 jit_solution(5120362713392717395)
XLA Ops:
  0.0 0.0 copy-start.1
  0.0 0.9 %copy-done.1 = f32[1,10,16,384]{3,2,1,0:T(8,128)S(1)} copy-done((f32[1,10,16,384]{3,2,1,0:T(8,128)S(1)}, f32[1,10,16,384]{3,2,1,0:T(8,128)}, u32[]{:S(2)}) %copy-start.1) | copy-done | bytes 245784
  0.9 0.0 copy-start.2
  0.9 0.0 copy-start.3
  0.9 0.0 copy-start.4
  1.0 0.0 copy-start.5
  1.0 14.1 %collective-permute-start.1 = (f32[160,256]{1,0:T(8,128)S(1)}, f32[160,256]{1,0:T(8,128)S(1)}, u32[]{:S(2)}, u32[]{:S(2)}) collective-permute-start(f32[160,256]{1,0:T(8,128)S(1)} %get-tuple-element.19), channel_id=1, source_target_pairs={{16,0},{32,16},{48,32},{64,48},{80,64},{96,80},{112,96},{128,112},... | collective-permute-start | bytes 491528 | tf_op jit(solution)/shard_map/ppermute | solution.py:323
  15.1 0.0 collective-permute-start
  15.1 0.0 copy-done.2
  15.1 0.0 copy-done.3
  15.1 0.0 copy-done.4
  15.1 0.0 copy-done.5
  15.1 3.3 %shard_map.65 = (s32[2,8,128]{2,1,0:T(8,128)S(1)}, f32[16,3,160,128]{3,2,1,0:T(8,128)S(1)}, f32[2,8,128]{2,1,0:T(8,128)S(1)}, f32[4,3,16,128]{3,2,1,0:T(8,128)S(...) custom-call(f32[160,384]{1,0:T(8,128)S(1)} %bitcast.21, ...), custom_call_target="tpu_custom_call" | custom-call | flops 1000000000 | tf_op jit(solution)/shard_map/pallas_call | solution.py:331
  18.5 0.0 collective-permute-done.1.right
  18.5 0.0 copy-start
  18.5 1.1 %collective-permute-done.left = f32[160,256]{1,0:T(8,128)S(1)} collective-permute-done((f32[160,256]{1,0:T(8,128)S(1)}, f32[160,256]{1,0:T(8,128)S(1)}, u32[]{:S(2)}, u32[]{:S(2)}) %collective-permute-start) | collective-permute-done | bytes 163872 | tf_op jit(solution)/shard_map/ppermute | solution.py:324
  19.6 0.0 copy-done
  19.6 2.5 %shard_map.67 = (f32[16,3,16,128]{3,2,1,0:T(8,128)S(1)}, f32[16,3,16,128]{3,2,1,0:T(8,128)S(1)}, f32[16,3,16,128]{3,2,1,0:T(8,128)S(1)}, f32[32,128]{1,0:T(8,128)S(1)}) custom-call(f32[160,256]{1,0:T(8,128)S(1)} %collective-permute-done.left, f32[160,256]{1,0:T(8,128)S(1)} %collective-permute-done.1.right, f32[16,384]{1,0:T(8,128)S(1)} %bitcast.18, ...), custom_call_target="tpu_custom_call" | custom-call | tf_op jit(solution)/shard_map/pallas_call | solution.py:352
  22.1 17.9 %all_to_all.22 = f32[32,1,128]{2,1,0:T(1,128)S(1)} all-to-all(f32[32,1,128]{2,1,0:T(1,128)S(1)} %bitcast.19), channel_id=1, replica_groups=mesh['sfc_0'=32,'sfc_1'=2,'lev_0'=4,'lev_1'=4] {'sfc_1','lev_0','lev_1'}, dimensions={0} | all-to-all | bytes 32768 | tf_op jit(solution)/shard_map/all_to_all | solution.py:362
  39.9 33.6 %all_to_all.23 = f32[32,1,128]{2,1,0:T(1,128)S(1)} all-to-all(f32[32,1,128]{2,1,0:T(1,128)S(1)} %bitcast.17), channel_id=1, replica_groups=mesh['sfc_0'=32,'sfc_1'=2,'lev_0'=4,'lev_1'=4] {'sfc_0'}, dimensions={0} | all-to-all | bytes 32768 | tf_op jit(solution)/shard_map/all_to_all | solution.py:364
  73.6 0.8 %shard_map.69 = f32[160,384]{1,0:T(8,128)} custom-call(f32[32,128]{1,0:T(8,128)S(1)} %bitcast.15, f32[16,3,16,128]{3,2,1,0:T(8,128)S(1)} %get-tuple-element.28.clip, f32[16,3,16,128]{3,2,1,0:T(8,128)S(1)} %get-tuple-element.29.up, f32[16,3,16,128]{3,2,1,0:T(8,128)S(1)} %get-tuple-element.30.down), custom_call_target="tpu_custom_call" | custom-call | tf_op jit(solution)/shard_map/pallas_call | solution.py:365
  (3 shorter events, 0.1 us)
Async XLA Ops:
  0.0 0.9 %copy-start.1 = (f32[1,10,16,384]{3,2,1,0:T(8,128)S(1)}, f32[1,10,16,384]{3,2,1,0:T(8,128)}, u32[]{:S(2)}) copy-start(f32[1,10,16,384]{3,2,1,0:T(8,128)} %param.6) | copy-start | bytes 737284
  0.9 14.2 %copy-start.2 = (f32[2,1,16,384]{3,2,1,0:T(8,128)S(1)}, f32[2,1,16,384]{3,2,1,0:T(8,128)}, u32[]{:S(2)}) copy-start(f32[2,1,16,384]{3,2,1,0:T(8,128)} %param.9) | copy-start | bytes 147460
  0.9 14.2 %copy-start.3 = (f32[1,16,384]{2,1,0:T(8,128)S(1)}, f32[1,16,384]{2,1,0:T(8,128)}, u32[]{:S(2)}) copy-start(f32[1,16,384]{2,1,0:T(8,128)} %param.7) | copy-start | bytes 73732
  0.9 14.2 %copy-start.4 = (s32[1,16,384]{2,1,0:T(8,128)S(1)}, s32[1,16,384]{2,1,0:T(8,128)}, u32[]{:S(2)}) copy-start(s32[1,16,384]{2,1,0:T(8,128)} %param.10) | copy-start | bytes 73732
  1.0 14.2 %copy-start.5 = (s32[1,2,128]{2,1,0:T(2,128)S(1)}, s32[1,2,128]{2,1,0:T(2,128)}, u32[]{:S(2)}) copy-start(s32[1,2,128]{2,1,0:T(2,128)} %param.11) | copy-start | bytes 3076
  1.0 17.5 %collective-permute-start.1 = (f32[160,256]{1,0:T(8,128)S(1)}, f32[160,256]{1,0:T(8,128)S(1)}, u32[]{:S(2)}, u32[]{:S(2)}) collective-permute-start(f32[160,256]{1,0:T(8,128)S(1)} %get-tuple-element.19), channel_id=1, source_target_pairs={{16,0},{32,16},{48,32},{64,48},{80,64},{96,80},{112,96},{128,112},... | collective-permute-start | bytes 491528 | tf_op jit(solution)/shard_map/ppermute | solution.py:323
  15.1 4.5 %collective-permute-start = (f32[160,256]{1,0:T(8,128)S(1)}, f32[160,256]{1,0:T(8,128)S(1)}, u32[]{:S(2)}, u32[]{:S(2)}) collective-permute-start(f32[160,256]{1,0:T(8,128)S(1)} %get-tuple-element.18), channel_id=1, source_target_pairs={{0,16},{16,32},{32,48},{48,64},{64,80},{80,96},{96,112},{112,128},... | collective-permute-start | bytes 491528 | tf_op jit(solution)/shard_map/ppermute | solution.py:324
  18.5 1.1 %copy-start = (f32[1,16,384]{2,1,0:T(8,128)S(1)}, f32[1,16,384]{2,1,0:T(8,128)}, u32[]{:S(2)}) copy-start(f32[1,16,384]{2,1,0:T(8,128)} %param.8) | copy-start | bytes 73732

commit v9 on v8

--- a/solution.py
+++ b/solution.py
@@ -101,8 +101,8 @@
 
 
 def own_part(
-    field, air_old, coord, slot, fetch,
-    picks, own_out, old_out, along_a, along_b, stacked, slots,
+    field, air_old, air_new, coord, slot, fetch,
+    picks, own_out, old_out, along_a, along_b, stacked, airs, slots,
     wide, table,
 ):
     chunks = slot.shape[1] // LANES
@@ -113,6 +113,7 @@
     for c in range(chunks):
         wide[c] = field[:, c * LANES : (c + 1) * LANES]
         slots[c] = slot[:, c * LANES : (c + 1) * LANES]
+        airs[c] = air_new[:, c * LANES : (c + 1) * LANES]
     for c in range(chunks):
         for v in range(REGISTERS):
             table[c, 8 * v : 8 * v + 8, :] = wide[c, rows(v), :]
@@ -172,25 +173,23 @@
 
 
 def last_part(
-    left, right, air_new, picks, merged, old, along_a, along_b, stacked, slots,
+    left, right, picks, own, merged, old, along_a, along_b, stacked, airs, slots,
     clip_out, up_out, down_out, sums_out,
-    wide, table, airs,
+    wide, table,
 ):
     points, chunks = merged.shape[:2]
     sub = lax.broadcasted_iota(jnp.int32, (8, LANES), 0)
     lane = lax.broadcasted_iota(jnp.int32, (8, LANES), 1)
     zero = jnp.zeros((8, LANES), jnp.float32)
-    for c in range(chunks):
-        airs[c] = air_new[:, c * LANES : (c + 1) * LANES]
-
-    def group(n, e, acc, sides):
+
+    def group(n, e, acc, sides, held):
         where = broadcast_row(slots, n, e)
         near, chunk = where & (LANES - 1), where >> 7
         masks = [(side, chunk == chunks + side) for side in sides]
 
         def value(v):
             at = slice(8 * v, 8 * v + 8)
-            x = merged[n, e, at, :]
+            x = held[n, e, at, :]
             for side, mask in masks:
                 x = jnp.where(mask, pick(table[side, at, :], near), x)
             return x
@@ -211,13 +210,13 @@
             acc[3 * h + 2] = acc[3 * h + 2] + air * down
         return tuple(acc)
 
-    def run(sides):
+    def run(sides, held):
         for side in sides:
             band_table((left, right)[side], picks[side], wide.at[side], table.at[side])
         acc = (old[0], zero, zero, old[1], zero, zero)
         for n in range(points):
             for e in range(chunks):
-                acc = group(n, e, acc, sides)
+                acc = group(n, e, acc, sides, held)
         row_of = zero
         for k in range(6):
             total = jnp.broadcast_to(jnp.sum(acc[k], axis=1, keepdims=True), (8, LANES))
@@ -233,11 +232,11 @@
 
     @pl.when(core == 0)
     def _():
-        run((0,))
+        run((0,), merged)
 
     @pl.when(core != 0)
     def _():
-        run((0, 1))
+        run((0, 1), own)
 
 
 def add_rows(parts):
@@ -287,7 +286,7 @@
         copy.wait()
 
 
-def in_vmem(kernel, out_shape, count, scratch=(), work=0, out_space=pltpu.VMEM, in_place=()):
+def in_vmem(kernel, out_shape, count, scratch=(), work=0, out_space=pltpu.VMEM):
     spec = pl.BlockSpec(memory_space=pltpu.VMEM)
     return pl.pallas_call(
         kernel,
@@ -295,7 +294,6 @@
         in_specs=[spec] * count,
         out_specs=jax.tree.map(lambda _: pl.BlockSpec(memory_space=out_space), out_shape),
         scratch_shapes=scratch,
-        input_output_aliases=dict(in_place),
         cost_estimate=pl.CostEstimate(flops=work, bytes_accessed=0, transcendentals=0),
         compiler_params=pltpu.CompilerParams(vmem_limit_bytes=GRANT),
     )
@@ -337,18 +335,17 @@
             terms,
             terms,
             shape(chunks, 8 * points, LANES),
+            shape(chunks, points, LANES),
             shape(chunks, points, LANES, dtype=whole),
         ),
-        5,
+        6,
         [
             pltpu.VMEM((chunks, tracers * points, LANES), real),
             pltpu.VMEM((chunks, 8 * REGISTERS, LANES), real),
         ],
         WORK,
-    )(field, air_old[0], dep_coord[:, 0], dep_slot[0], fetch_list[0])
-    merged = in_vmem(right_part, picked, 4, [wide, table], WORK, in_place=((2, 0),))(
-        right, picks, own, rest[-1]
-    )
+    )(field, air_old[0], air_new[0], dep_coord[:, 0], dep_slot[0], fetch_list[0])
+    merged = in_vmem(right_part, picked, 4, [wide, table], WORK)(right, picks, own, rest[-1])
     clip, up, down, sums = in_vmem(
         last_part,
         (mid, mid, mid, shape(plane, LANES)),
@@ -356,9 +353,8 @@
         [
             pltpu.VMEM((2, 2, tracers * points, LANES), real),
             pltpu.VMEM((2, 8 * REGISTERS, LANES), real),
-            pltpu.VMEM((chunks, points, LANES), real),
         ],
-    )(left, right, air_new[0], picks, merged, *rest)
+    )(left, right, picks, own, merged, *rest)
     sums = lax.all_to_all(sums, PLANE, 0, 0, tiled=True)
     sums = in_vmem(relay, shape(line, LANES), 1)(sums)
     sums = lax.all_to_all(sums, LINE, 0, 0, tiled=True)

time: 74.6 us -> 74.4 us (level)
  transfers between devices with their start and end apart: 2 -> 2, of which waited for: 1 -> 1; matrix products, arithmetic and copies ran while one was open for 0% -> 0% of each run, Pallas kernels for 4% -> 5%
where the time goes in v9:
time: 74.4 us; the launch traced here: 74.2 us
  blocking collectives  51.2 us (69%)
  starting transfers between devices  14.1 us (19%)
  Pallas kernels  6.73 us (9%)
  waiting for transfers between devices  1.07 us (1%)
  local copies, waits for them, and re-layouts  0.96 us (1%)
    all_to_all x1, blocking collectives, on_device(): sums = lax.all_to_all(sums, LINE, 0, 0, tiled=True)  33.3 us
    all_to_all x1, blocking collectives, on_device(): sums = lax.all_to_all(sums, PLANE, 0, 0, tiled=True)  17.9 us
    ppermute x1, starting transfers between devices, on_device(): right = lax.ppermute(first, SFC, backward)  14.1 us
    pallas_call x1, Pallas kernels, on_device(): in_vmem(own_part, (shape(2, 8, LANES, dtype=whole), picked, shape(2, 8, L...  3.33 us
    pallas_call x1, Pallas kernels, on_device(): in_vmem(last_part, (mid, mid, mid, shape(plane, LANES)), 5 + len(rest), [...  2.5 us
  transfers between devices with their start and end apart: 2, of which 1 were waited for; matrix products, arithmetic and copies ran while one was open for 0% of the time, Pallas kernels for 5%

profile of v9, /device:TPU:1, one launch (start us, length us, event | category | flops | bytes accessed | tf_op | source)
XLA Modules:
  0.0 74.2 jit_solution(6945524662517927921)
XLA Ops:
  0.0 0.0 copy-start
  0.0 0.9 %copy-done = f32[1,10,16,384]{3,2,1,0:T(8,128)S(1)} copy-done((f32[1,10,16,384]{3,2,1,0:T(8,128)S(1)}, f32[1,10,16,384]{3,2,1,0:T(8,128)}, u32[]{:S(2)}) %copy-start) | copy-done | bytes 245784
  0.9 0.0 copy-start.1
  0.9 0.0 copy-start.2
  0.9 0.0 copy-start.3
  1.0 0.0 copy-start.4
  1.0 0.0 copy-start.5
  1.0 14.1 %collective-permute-start.1 = (f32[160,256]{1,0:T(8,128)S(1)}, f32[160,256]{1,0:T(8,128)S(1)}, u32[]{:S(2)}, u32[]{:S(2)}) collective-permute-start(f32[160,256]{1,0:T(8,128)S(1)} %get-tuple-element.20), channel_id=1, source_target_pairs={{16,0},{32,16},{48,32},{64,48},{80,64},{96,80},{112,96},{128,112},... | collective-permute-start | bytes 491528 | tf_op jit(solution)/shard_map/ppermute | solution.py:321
  15.1 0.0 collective-permute-start
  15.1 0.0 copy-done.1
  15.1 0.0 copy-done.2
  15.1 0.0 copy-done.3
  15.1 0.0 copy-done.4
  15.2 0.0 copy-done.5
  15.2 3.3 %shard_map.65 = (s32[2,8,128]{2,1,0:T(8,128)S(1)}, f32[16,3,160,128]{3,2,1,0:T(8,128)S(1)}, f32[2,8,128]{2,1,0:T(8,128)S(1)}, f32[4,3,16,128]{3,2,1,0:T(8,128)S(...) custom-call(f32[160,384]{1,0:T(8,128)S(1)} %bitcast.20, ...), custom_call_target="tpu_custom_call" | custom-call | flops 1000000000 | tf_op jit(solution)/shard_map/pallas_call | solution.py:329
  18.5 0.0 collective-permute-done.1.right
  18.5 1.1 %collective-permute-done.left = f32[160,256]{1,0:T(8,128)S(1)} collective-permute-done((f32[160,256]{1,0:T(8,128)S(1)}, f32[160,256]{1,0:T(8,128)S(1)}, u32[]{:S(2)}, u32[]{:S(2)}) %collective-permute-start) | collective-permute-done | bytes 163872 | tf_op jit(solution)/shard_map/ppermute | solution.py:322
  19.6 2.5 %shard_map.67 = (f32[16,3,16,128]{3,2,1,0:T(8,128)S(1)}, f32[16,3,16,128]{3,2,1,0:T(8,128)S(1)}, f32[16,3,16,128]{3,2,1,0:T(8,128)S(1)}, f32[32,128]{1,0:T(8,128)S(1)}) custom-call(f32[160,256]{1,0:T(8,128)S(1)} %collective-permute-done.left, f32[160,256]{1,0:T(8,128)S(1)} %collective-permute-done.1.right, s32[2,8,128]{2,1,0:T(8,128)S(1)} %get-tuple-element.21.picks, ...), custom_call_target="tpu_custom_call" | custom-call | tf_op jit(solution)/shard_map/pallas_call | solution.py:349
  22.1 17.9 %all_to_all.22 = f32[32,1,128]{2,1,0:T(1,128)S(1)} all-to-all(f32[32,1,128]{2,1,0:T(1,128)S(1)} %bitcast.18), channel_id=1, replica_groups=mesh['sfc_0'=32,'sfc_1'=2,'lev_0'=4,'lev_1'=4] {'sfc_1','lev_0','lev_1'}, dimensions={0} | all-to-all | bytes 32768 | tf_op jit(solution)/shard_map/all_to_all | solution.py:358
  40.0 33.3 %all_to_all.23 = f32[32,1,128]{2,1,0:T(1,128)S(1)} all-to-all(f32[32,1,128]{2,1,0:T(1,128)S(1)} %bitcast.17), channel_id=1, replica_groups=mesh['sfc_0'=32,'sfc_1'=2,'lev_0'=4,'lev_1'=4] {'sfc_0'}, dimensions={0} | all-to-all | bytes 32768 | tf_op jit(solution)/shard_map/all_to_all | solution.py:360
  73.3 0.8 %shard_map.69 = f32[160,384]{1,0:T(8,128)} custom-call(f32[32,128]{1,0:T(8,128)S(1)} %bitcast.15, f32[16,3,16,128]{3,2,1,0:T(8,128)S(1)} %get-tuple-element.30.clip, f32[16,3,16,128]{3,2,1,0:T(8,128)S(1)} %get-tuple-element.31.up, f32[16,3,16,128]{3,2,1,0:T(8,128)S(1)} %get-tuple-element.32.down), custom_call_target="tpu_custom_call" | custom-call | tf_op jit(solution)/shard_map/pallas_call | solution.py:361
  (3 shorter events, 0.1 us)
Async XLA Ops:
  0.0 0.9 %copy-start = (f32[1,10,16,384]{3,2,1,0:T(8,128)S(1)}, f32[1,10,16,384]{3,2,1,0:T(8,128)}, u32[]{:S(2)}) copy-start(f32[1,10,16,384]{3,2,1,0:T(8,128)} %param.6) | copy-start | bytes 737284
  0.9 14.2 %copy-start.1 = (f32[2,1,16,384]{3,2,1,0:T(8,128)S(1)}, f32[2,1,16,384]{3,2,1,0:T(8,128)}, u32[]{:S(2)}) copy-start(f32[2,1,16,384]{3,2,1,0:T(8,128)} %param.9) | copy-start | bytes 147460
  0.9 14.2 %copy-start.2 = (f32[1,16,384]{2,1,0:T(8,128)S(1)}, f32[1,16,384]{2,1,0:T(8,128)}, u32[]{:S(2)}) copy-start(f32[1,16,384]{2,1,0:T(8,128)} %param.7) | copy-start | bytes 73732
  0.9 14.2 %copy-start.3 = (f32[1,16,384]{2,1,0:T(8,128)S(1)}, f32[1,16,384]{2,1,0:T(8,128)}, u32[]{:S(2)}) copy-start(f32[1,16,384]{2,1,0:T(8,128)} %param.8) | copy-start | bytes 73732
  1.0 14.2 %copy-start.4 = (s32[1,16,384]{2,1,0:T(8,128)S(1)}, s32[1,16,384]{2,1,0:T(8,128)}, u32[]{:S(2)}) copy-start(s32[1,16,384]{2,1,0:T(8,128)} %param.10) | copy-start | bytes 73732
  1.0 14.2 %copy-start.5 = (s32[1,2,128]{2,1,0:T(2,128)S(1)}, s32[1,2,128]{2,1,0:T(2,128)}, u32[]{:S(2)}) copy-start(s32[1,2,128]{2,1,0:T(2,128)} %param.11) | copy-start | bytes 3076
  1.0 17.5 %collective-permute-start.1 = (f32[160,256]{1,0:T(8,128)S(1)}, f32[160,256]{1,0:T(8,128)S(1)}, u32[]{:S(2)}, u32[]{:S(2)}) collective-permute-start(f32[160,256]{1,0:T(8,128)S(1)} %get-tuple-element.20), channel_id=1, source_target_pairs={{16,0},{32,16},{48,32},{64,48},{80,64},{96,80},{112,96},{128,112},... | collective-permute-start | bytes 491528 | tf_op jit(solution)/shard_map/ppermute | solution.py:321
  15.1 4.5 %collective-permute-start = (f32[160,256]{1,0:T(8,128)S(1)}, f32[160,256]{1,0:T(8,128)S(1)}, u32[]{:S(2)}, u32[]{:S(2)}) collective-permute-start(f32[160,256]{1,0:T(8,128)S(1)} %get-tuple-element.19), channel_id=1, source_target_pairs={{0,16},{16,32},{32,48},{48,64},{64,80},{80,96},{96,112},{112,128},... | collective-permute-start | bytes 491528 | tf_op jit(solution)/shard_map/ppermute | solution.py:322

commit v10 on v9

--- a/solution.py
+++ b/solution.py
@@ -146,22 +146,20 @@
             stacked[c, pl.ds(i + 4, points, stride=8), :] = terms_a[i][:, cols]
 
 
-def band_table(band, idx, wide, table):
-    for c in range(2):
-        wide[c] = band[:, c * LANES : (c + 1) * LANES]
+def band_table(band, idx, table):
     near, far = idx & (LANES - 1), idx >= LANES
     for v in range(REGISTERS):
-        first = pick(wide[0, rows(v), :], near)
-        second = pick(wide[1, rows(v), :], near)
+        first = pick(band[0, rows(v), :], near)
+        second = pick(band[1, rows(v), :], near)
         table[8 * v : 8 * v + 8, :] = jnp.where(far, second, first)
 
 
-def right_part(right, picks, own, slots, merged_out, wide, table):
+def right_part(right, picks, own, slots, merged_out, table):
     points, chunks = own.shape[:2]
 
     @pl.when(lax.axis_index("sfc_1") == 0)
     def _():
-        band_table(right, picks[1], wide, table)
+        band_table(right, picks[1], table)
         for n in range(points):
             for e in range(chunks):
                 where = broadcast_row(slots, n, e)
@@ -175,7 +173,7 @@
 def last_part(
     left, right, picks, own, merged, old, along_a, along_b, stacked, airs, slots,
     clip_out, up_out, down_out, sums_out,
-    wide, table,
+    table,
 ):
     points, chunks = merged.shape[:2]
     sub = lax.broadcasted_iota(jnp.int32, (8, LANES), 0)
@@ -212,7 +210,7 @@
 
     def run(sides, held):
         for side in sides:
-            band_table((left, right)[side], picks[side], wide.at[side], table.at[side])
+            band_table((left, right)[side], picks[side], table.at[side])
         acc = (old[0], zero, zero, old[1], zero, zero)
         for n in range(points):
             for e in range(chunks):
@@ -300,8 +298,9 @@
 
 
 def bands(field, last_out, first_out):
-    last_out[...] = field[:, field.shape[1] - BAND :]
-    first_out[...] = field[:, :BAND]
+    for out, start in ((last_out, field.shape[1] - BAND), (first_out, 0)):
+        for c in range(BAND // LANES):
+            out[c] = field[:, start + c * LANES : start + (c + 1) * LANES]
 
 
 def on_device(tracer_old, air_old, air_new, dep_coord, dep_slot, fetch_list):
@@ -313,7 +312,7 @@
     def shape(*dims, dtype=real):
         return jax.ShapeDtypeStruct(dims, dtype)
 
-    band = shape(tracers * points, BAND)
+    band = shape(BAND // LANES, tracers * points, LANES)
     last, first = in_vmem(bands, (band, band), 1, work=LOAD)(field)
     count = lax.axis_size(SFC)
     forward = [(i, (i + 1) % count) for i in range(count)]
@@ -324,7 +323,6 @@
     plane, line = lax.axis_size(PLANE), lax.axis_size(LINE)
     terms = shape(4, chunks, points, LANES)
     table = pltpu.VMEM((8 * REGISTERS, LANES), real)
-    wide = pltpu.VMEM((2, tracers * points, LANES), real)
     picked = shape(points, chunks, 8 * REGISTERS, LANES)
     picks, own, *rest = in_vmem(
         own_part,
@@ -345,15 +343,12 @@
         ],
         WORK,
     )(field, air_old[0], air_new[0], dep_coord[:, 0], dep_slot[0], fetch_list[0])
-    merged = in_vmem(right_part, picked, 4, [wide, table], WORK)(right, picks, own, rest[-1])
+    merged = in_vmem(right_part, picked, 4, [table], WORK)(right, picks, own, rest[-1])
     clip, up, down, sums = in_vmem(
         last_part,
         (mid, mid, mid, shape(plane, LANES)),
         5 + len(rest),
-        [
-            pltpu.VMEM((2, 2, tracers * points, LANES), real),
-            pltpu.VMEM((2, 8 * REGISTERS, LANES), real),
-        ],
+        [pltpu.VMEM((2, 8 * REGISTERS, LANES), real)],
     )(left, right, picks, own, merged, *rest)
     sums = lax.all_to_all(sums, PLANE, 0, 0, tiled=True)
     sums = in_vmem(relay, shape(line, LANES), 1)(sums)

time: 74.4 us -> 74.4 us (level)
  no operation moved by 1% of the time
where the time goes in v10:
time: 74.4 us; the launch traced here: 74.1 us
  blocking collectives  51.2 us (69%)
  starting transfers between devices  14.1 us (19%)
  Pallas kernels  6.7 us (9%)
  waiting for transfers between devices  1.07 us (1%)
  local copies, waits for them, and re-layouts  0.96 us (1%)
    all_to_all x1, blocking collectives, on_device(): sums = lax.all_to_all(sums, LINE, 0, 0, tiled=True)  33.3 us
    all_to_all x1, blocking collectives, on_device(): sums = lax.all_to_all(sums, PLANE, 0, 0, tiled=True)  17.9 us
    ppermute x1, starting transfers between devices, on_device(): right = lax.ppermute(first, SFC, backward)  14.1 us
    pallas_call x1, Pallas kernels, on_device(): in_vmem(own_part, (shape(2, 8, LANES, dtype=whole), picked, shape(2, 8, L...  3.33 us
    pallas_call x1, Pallas kernels, on_device(): in_vmem(last_part, (mid, mid, mid, shape(plane, LANES)), 5 + len(rest), [...  2.48 us
  transfers between devices with their start and end apart: 2, of which 1 were waited for; matrix products, arithmetic and copies ran while one was open for 0% of the time, Pallas kernels for 5%

profile of v10, /device:TPU:1, one launch (start us, length us, event | category | flops | bytes accessed | tf_op | source)
XLA Modules:
  0.0 74.1 jit_solution(16752177895563716931)
XLA Ops:
  0.0 0.0 copy-start
  0.0 0.9 %copy-done = f32[1,10,16,384]{3,2,1,0:T(8,128)S(1)} copy-done((f32[1,10,16,384]{3,2,1,0:T(8,128)S(1)}, f32[1,10,16,384]{3,2,1,0:T(8,128)}, u32[]{:S(2)}) %copy-start) | copy-done | bytes 245784
  0.9 0.0 copy-start.1
  0.9 0.0 copy-start.2
  0.9 0.0 copy-start.3
  1.0 0.0 copy-start.4
  1.0 0.0 copy-start.5
  1.0 14.1 %collective-permute-start.1 = (f32[2,160,128]{2,1,0:T(8,128)S(1)}, f32[2,160,128]{2,1,0:T(8,128)S(1)}, u32[]{:S(2)}, u32[]{:S(2)}) collective-permute-start(f32[2,160,128]{2,1,0:T(8,128)S(1)} %get-tuple-element.20), channel_id=1, source_target_pairs={{16,0},{32,16},{48,32},{64,48},{80,64},{96,80},{112,96},{128,112},... | collective-permute-start | bytes 491528 | tf_op jit(solution)/shard_map/ppermute | solution.py:320
  15.1 0.0 collective-permute-start
  15.1 0.0 copy-done.1
  15.1 0.0 copy-done.2
  15.1 0.0 copy-done.3
  15.1 0.0 copy-done.4
  15.2 0.0 copy-done.5
  15.2 3.3 %shard_map.65 = (s32[2,8,128]{2,1,0:T(8,128)S(1)}, f32[16,3,160,128]{3,2,1,0:T(8,128)S(1)}, f32[2,8,128]{2,1,0:T(8,128)S(1)}, f32[4,3,16,128]{3,2,1,0:T(8,128)S(...) custom-call(f32[160,384]{1,0:T(8,128)S(1)} %bitcast.20, ...), custom_call_target="tpu_custom_call" | custom-call | flops 1000000000 | tf_op jit(solution)/shard_map/pallas_call | solution.py:327
  18.5 0.0 collective-permute-done.1.right
  18.5 1.1 %collective-permute-done.left = f32[2,160,128]{2,1,0:T(8,128)S(1)} collective-permute-done((f32[2,160,128]{2,1,0:T(8,128)S(1)}, f32[2,160,128]{2,1,0:T(8,128)S(1)}, u32[]{:S(2)}, u32[]{:S(2)}) %collective-permute-start) | collective-permute-done | bytes 163872 | tf_op jit(solution)/shard_map/ppermute | solution.py:321
  19.6 2.5 %shard_map.67 = (f32[16,3,16,128]{3,2,1,0:T(8,128)S(1)}, f32[16,3,16,128]{3,2,1,0:T(8,128)S(1)}, f32[16,3,16,128]{3,2,1,0:T(8,128)S(1)}, f32[32,128]{1,0:T(8,128)S(1)}) custom-call(f32[2,160,128]{2,1,0:T(8,128)S(1)} %collective-permute-done.left, f32[2,160,128]{2,1,0:T(8,128)S(1)} %collective-permute-done.1.right, s32[2,8,128]{2,1,0:T(8,128)S(1)} %get-tuple-element.21.picks, ...), custom_call_target="tpu_custom_call" | custom-call | tf_op jit(solution)/shard_map/pallas_call | solution.py:347
  22.1 17.9 %all_to_all.22 = f32[32,1,128]{2,1,0:T(1,128)S(1)} all-to-all(f32[32,1,128]{2,1,0:T(1,128)S(1)} %bitcast.18), channel_id=1, replica_groups=mesh['sfc_0'=32,'sfc_1'=2,'lev_0'=4,'lev_1'=4] {'sfc_1','lev_0','lev_1'}, dimensions={0} | all-to-all | bytes 32768 | tf_op jit(solution)/shard_map/all_to_all | solution.py:353
  40.0 33.3 %all_to_all.23 = f32[32,1,128]{2,1,0:T(1,128)S(1)} all-to-all(f32[32,1,128]{2,1,0:T(1,128)S(1)} %bitcast.17), channel_id=1, replica_groups=mesh['sfc_0'=32,'sfc_1'=2,'lev_0'=4,'lev_1'=4] {'sfc_0'}, dimensions={0} | all-to-all | bytes 32768 | tf_op jit(solution)/shard_map/all_to_all | solution.py:355
  73.3 0.8 %shard_map.69 = f32[160,384]{1,0:T(8,128)} custom-call(f32[32,128]{1,0:T(8,128)S(1)} %bitcast.15, f32[16,3,16,128]{3,2,1,0:T(8,128)S(1)} %get-tuple-element.30.clip, f32[16,3,16,128]{3,2,1,0:T(8,128)S(1)} %get-tuple-element.31.up, f32[16,3,16,128]{3,2,1,0:T(8,128)S(1)} %get-tuple-element.32.down), custom_call_target="tpu_custom_call" | custom-call | tf_op jit(solution)/shard_map/pallas_call | solution.py:356
  (3 shorter events, 0.1 us)
Async XLA Ops:
  0.0 0.9 %copy-start = (f32[1,10,16,384]{3,2,1,0:T(8,128)S(1)}, f32[1,10,16,384]{3,2,1,0:T(8,128)}, u32[]{:S(2)}) copy-start(f32[1,10,16,384]{3,2,1,0:T(8,128)} %param.6) | copy-start | bytes 737284
  0.9 14.2 %copy-start.1 = (f32[2,1,16,384]{3,2,1,0:T(8,128)S(1)}, f32[2,1,16,384]{3,2,1,0:T(8,128)}, u32[]{:S(2)}) copy-start(f32[2,1,16,384]{3,2,1,0:T(8,128)} %param.9) | copy-start | bytes 147460
  0.9 14.2 %copy-start.2 = (f32[1,16,384]{2,1,0:T(8,128)S(1)}, f32[1,16,384]{2,1,0:T(8,128)}, u32[]{:S(2)}) copy-start(f32[1,16,384]{2,1,0:T(8,128)} %param.7) | copy-start | bytes 73732
  0.9 14.2 %copy-start.3 = (f32[1,16,384]{2,1,0:T(8,128)S(1)}, f32[1,16,384]{2,1,0:T(8,128)}, u32[]{:S(2)}) copy-start(f32[1,16,384]{2,1,0:T(8,128)} %param.8) | copy-start | bytes 73732
  1.0 14.2 %copy-start.4 = (s32[1,16,384]{2,1,0:T(8,128)S(1)}, s32[1,16,384]{2,1,0:T(8,128)}, u32[]{:S(2)}) copy-start(s32[1,16,384]{2,1,0:T(8,128)} %param.10) | copy-start | bytes 73732
  1.0 14.2 %copy-start.5 = (s32[1,2,128]{2,1,0:T(2,128)S(1)}, s32[1,2,128]{2,1,0:T(2,128)}, u32[]{:S(2)}) copy-start(s32[1,2,128]{2,1,0:T(2,128)} %param.11) | copy-start | bytes 3076
  1.0 17.5 %collective-permute-start.1 = (f32[2,160,128]{2,1,0:T(8,128)S(1)}, f32[2,160,128]{2,1,0:T(8,128)S(1)}, u32[]{:S(2)}, u32[]{:S(2)}) collective-permute-start(f32[2,160,128]{2,1,0:T(8,128)S(1)} %get-tuple-element.20), channel_id=1, source_target_pairs={{16,0},{32,16},{48,32},{64,48},{80,64},{96,80},{112,96},{128,112},... | collective-permute-start | bytes 491528 | tf_op jit(solution)/shard_map/ppermute | solution.py:320
  15.1 4.5 %collective-permute-start = (f32[2,160,128]{2,1,0:T(8,128)S(1)}, f32[2,160,128]{2,1,0:T(8,128)S(1)}, u32[]{:S(2)}, u32[]{:S(2)}) collective-permute-start(f32[2,160,128]{2,1,0:T(8,128)S(1)} %get-tuple-element.19), channel_id=1, source_target_pairs={{0,16},{16,32},{32,48},{48,64},{64,80},{80,96},{96,112},{112,128},... | collective-permute-start | bytes 491528 | tf_op jit(solution)/shard_map/ppermute | solution.py:321
